TPU v7x, 32 devices: a whole 2x2x4 slice. The times are simulated.
32 devices in a mesh: tp: 4 (over z), dp: 8 (over y, x, core).
Axes of the slice: x: 2, y: 2, z: 4, core: 2. Of those that a mesh axis runs over, the one named last changes fastest.
Arguments:
- x_in: bfloat16 [2048, 4096], P(('dp', 'tp'))
- w_gate: bfloat16 [4096, 14336], P('dp', 'tp')
- w_up: bfloat16 [4096, 14336], P('dp', 'tp')
- w_down: bfloat16 [14336, 4096], P('tp', 'dp')
- grad_y: bfloat16 [2048, 4096], P(('dp', 'tp'))
Outputs:
- output 1: bfloat16 [2048, 4096], P(('dp', 'tp'))
- output 2: bfloat16 [2048, 4096], P(('dp', 'tp'))
- output 3: float32 [4096, 14336], P('dp', 'tp')
- output 4: float32 [4096, 14336], P('dp', 'tp')
- output 5: float32 [14336, 4096], P('tp', 'dp')
All inputs are finite; a program needn't handle non-finite values.
Results may differ from a plain program's by a relative error of at most 0.001.
Values are sent between devices in bfloat16 or wider.
A program may use at most 1 GiB of HBM per device.

v0:
```python
import jax
import jax.numpy as jnp
from jax import lax
from jax.sharding import PartitionSpec as P


def solution(mesh):
    dp_size = mesh.shape["dp"]
    tp_size = mesh.shape["tp"]

    def spread_cols(rows_loc):
        tok_dev = rows_loc.shape[0]
        cols_mine = lax.all_to_all(rows_loc, "dp", 1, 0, tiled=True)
        col_width = cols_mine.shape[1]
        cols_mine = cols_mine.reshape(dp_size, tok_dev, col_width)
        gathered = lax.all_gather(cols_mine, "tp", axis=1)
        return cols_mine, gathered.reshape(dp_size * tp_size * tok_dev, col_width)

    def collect_rows(col_part, resid):
        tok_dev = resid.shape[1]
        col_width = col_part.shape[1]
        summed = lax.psum_scatter(col_part.reshape(dp_size, tp_size, tok_dev, col_width), "tp", scatter_dimension=1, tiled=True)
        summed = summed.reshape(dp_size, tok_dev, col_width) + resid.astype(jnp.float32)
        out_rows = lax.all_to_all(summed.astype(jnp.bfloat16), "dp", 0, 2, tiled=True)
        return out_rows.reshape(tok_dev, dp_size * col_width)

    def local_step(x_loc, wg_loc, wu_loc, wd_loc, gy_loc):
        x_mine, x_cols = spread_cols(x_loc)
        gate_pre = lax.psum_scatter(jnp.dot(x_cols, wg_loc, preferred_element_type=jnp.float32), "dp", scatter_dimension=0, tiled=True)
        up_pre = lax.psum_scatter(jnp.dot(x_cols, wu_loc, preferred_element_type=jnp.float32), "dp", scatter_dimension=0, tiled=True)
        sig_gate = jax.nn.sigmoid(gate_pre)
        silu_gate = gate_pre * sig_gate
        hidden = (silu_gate * up_pre).astype(jnp.bfloat16)
        hidden_all = lax.all_gather(hidden, "dp", axis=0, tiled=True)
        y_rows = collect_rows(jnp.dot(hidden_all, wd_loc, preferred_element_type=jnp.float32), x_mine)

        gy_mine, gy_cols = spread_cols(gy_loc)
        grad_h = lax.psum_scatter(jnp.einsum("nd,fd->nf", gy_cols, wd_loc, preferred_element_type=jnp.float32), "dp", scatter_dimension=0, tiled=True)
        grad_wd = jnp.einsum("nf,nd->fd", hidden_all, gy_cols, preferred_element_type=jnp.float32)
        silu_deriv = sig_gate * (1.0 + gate_pre * (1.0 - sig_gate))
        grad_gate = (grad_h * up_pre * silu_deriv).astype(jnp.bfloat16)
        grad_up = (grad_h * silu_gate).astype(jnp.bfloat16)
        gate_all = lax.all_gather(grad_gate, "dp", axis=0, tiled=True)
        up_all = lax.all_gather(grad_up, "dp", axis=0, tiled=True)
        grad_wg = jnp.einsum("nd,nf->df", x_cols, gate_all, preferred_element_type=jnp.float32)
        grad_wu = jnp.einsum("nd,nf->df", x_cols, up_all, preferred_element_type=jnp.float32)
        gx_part = (jnp.einsum("nf,df->nd", gate_all, wg_loc, preferred_element_type=jnp.float32)
                   + jnp.einsum("nf,df->nd", up_all, wu_loc, preferred_element_type=jnp.float32))
        gx_rows = collect_rows(gx_part, gy_mine)
        return y_rows, gx_rows, grad_wg, grad_wu, grad_wd

    row_spec = P(("dp", "tp"), None)
    up_spec = P("dp", "tp")
    down_spec = P("tp", "dp")
    return jax.shard_map(local_step, mesh=mesh,
                         in_specs=(row_spec, up_spec, up_spec, down_spec, row_spec),
                         out_specs=(row_spec, row_spec, up_spec, up_spec, down_spec),
                         check_vma=False)
```

profile of v0, /device:TPU:0, one launch (start us, length us, event | category | flops | bytes accessed | tf_op | source)
XLA Modules:
  0.0 1292.5 jit_solution(16965632937203596460)
XLA Ops:
  7.2 1.1 copy.50
  8.4 14.7 %all_to_all.62 = bf16[64,8,512]{2,0,1:T(8,128)(2,1)S(1)} all-to-all(bf16[64,8,512]{2,0,1:T(8,128)(2,1)S(1)} %bitcast.91), channel_id=1, replica_groups=mesh['tp'=4,'dp'=8] {'dp'}, dimensions={1} | all-to-all | bytes 1048576 | tf_op jit(solution)/shard_map/all_to_all | solution.py:13
  23.1 1.1 copy.33
  24.3 12.1 all_to_all.63
  38.4 31.0 %all-gather.16.cloned.1.call-done = bf16[8,256,512]{2,0,1:T(8,128)(2,1)} async-done(((bf16[8,64,512]{2,0,1:T(8,128)(2,1)}), bf16[8,256,512]{2,0,1:T(8,128)(2,1)}) %all-gather.16.cloned.1.call-update) | async-done | bytes 2097168 | tf_op jit(solution)/shard_map/all_gather | solution.py:16
  69.4 2.4 copy.34
  71.8 1.3 copy-done.2
  73.1 13.8 %fusion.8 = f32[2048,3584]{1,0:T(8,128)} fusion(bf16[2048,512]{1,0:T(8,128)(2,1)S(1)} %bitcast.87, bf16[3584,512]{1,0:T(8,128)(2,1)S(1)} %copy-done.4), kind=kOutput, calls=%fused_computation.19 | convolution fusion | flops 7516192768 | bytes 35127296 | tf_op jit(solution)/shard_map/nd,fd->nf/dot_general | solution.py:38
  86.9 29.0 %all-gather.14.cloned.1.call-done = bf16[8,256,512]{2,0,1:T(8,128)(2,1)} async-done(((bf16[8,64,512]{2,0,1:T(8,128)(2,1)}), bf16[8,256,512]{2,0,1:T(8,128)(2,1)}) %all-gather.14.cloned.1.call-update) | async-done | bytes 2097168 | tf_op jit(solution)/shard_map/all_gather | solution.py:16
  116.0 2.4 copy.30
  118.7 19.6 %fusion.6 = f32[2048,3584]{1,0:T(8,128)} fusion(bf16[2048,512]{1,0:T(8,128)(2,1)S(1)} %bitcast.83, bf16[512,3584]{1,0:T(8,128)(2,1)S(1)} %copy-done.5), kind=kOutput, calls=%fused_computation.17 | convolution fusion | flops 7516192768 | bytes 35127296 | tf_op jit(solution)/shard_map/dot_general | solution.py:30
  138.5 21.6 %fusion.5 = f32[2048,3584]{1,0:T(8,128)} fusion(bf16[2048,512]{1,0:T(8,128)(2,1)S(1)} %bitcast.84, bf16[512,3584]{1,0:T(8,128)(2,1)} %param.6), kind=kOutput, calls=%fused_computation.16 | convolution fusion | flops 7516192768 | bytes 35127296 | tf_op jit(solution)/shard_map/dot_general | solution.py:29
  160.2 139.2 %reduce-scatter.14.cloned.1.call-done = f32[256,3584]{1,0:T(8,128)} async-done(((f32[2048,3584]{1,0:T(8,128)}), f32[256,3584]{1,0:T(8,128)}) %reduce-scatter.14.cloned.1.call-update) | async-done | bytes 3670032 | tf_op jit(solution)/shard_map/reduce_scatter | solution.py:38
  299.4 184.5 %reduce-scatter.12.cloned.1.call-done = f32[256,3584]{1,0:T(8,128)} async-done(((f32[2048,3584]{1,0:T(8,128)}), f32[256,3584]{1,0:T(8,128)}) %reduce-scatter.12.cloned.1.call-update) | async-done | bytes 3670032 | tf_op jit(solution)/shard_map/reduce_scatter | solution.py:30
  483.9 184.5 %reduce-scatter.10.cloned.1.call-done = f32[256,3584]{1,0:T(8,128)} async-done(((f32[2048,3584]{1,0:T(8,128)}), f32[256,3584]{1,0:T(8,128)}) %reduce-scatter.10.cloned.1.call-update) | async-done | bytes 3670032 | tf_op jit(solution)/shard_map/reduce_scatter | solution.py:29
  668.4 6.8 multiply_convert_fusion
  676.8 79.5 %all-gather.8.cloned.1.call-done = bf16[2048,3584]{1,0:T(8,128)(2,1)} async-done(((bf16[256,3584]{1,0:T(8,128)(2,1)}), bf16[2048,3584]{1,0:T(8,128)(2,1)}) %all-gather.8.cloned.1.call-update) | async-done | bytes 14680080 | tf_op jit(solution)/shard_map/all_gather | solution.py:34
  756.2 13.3 %fusion.7 = f32[2048,512]{1,0:T(8,128)} fusion(bf16[2048,3584]{1,0:T(8,128)(2,1)} %all-gather.8.cloned.1.call-done, bf16[3584,512]{1,0:T(8,128)(2,1)} %param.8), kind=kOutput, calls=%fused_computation.18 | convolution fusion | flops 7516192768 | bytes 22544384 | tf_op jit(solution)/shard_map/dot_general | solution.py:35
  769.6 70.0 %all-gather.10.cloned.1.call-done = bf16[2048,3584]{1,0:T(8,128)(2,1)} async-done(((bf16[256,3584]{1,0:T(8,128)(2,1)}), bf16[2048,3584]{1,0:T(8,128)(2,1)}) %all-gather.10.cloned.1.call-update) | async-done | bytes 14680080 | tf_op jit(solution)/shard_map/all_gather | solution.py:43
  839.6 13.4 %fusion.9 = f32[2048,512]{1,0:T(8,128)} fusion(bf16[2048,3584]{1,0:T(8,128)(2,1)} %all-gather.10.cloned.1.call-done, bf16[512,3584]{1,0:T(8,128)(2,1)} %param.6), kind=kOutput, calls=%fused_computation.20 | convolution fusion | flops 7516192768 | bytes 22544384 | tf_op jit(solution)/shard_map/nf,df->nd/dot_general | solution.py:47
  853.0 70.0 %all-gather.12.cloned.1.call-done = bf16[2048,3584]{1,0:T(8,128)(2,1)} async-done(((bf16[256,3584]{1,0:T(8,128)(2,1)}), bf16[2048,3584]{1,0:T(8,128)(2,1)}) %all-gather.12.cloned.1.call-update) | async-done | bytes 14680080 | tf_op jit(solution)/shard_map/all_gather | solution.py:44
  922.9 14.0 %convolution_add_fusion = f32[2048,512]{1,0:T(8,128)} fusion(f32[2048,512]{1,0:T(8,128)} %fusion.9, bf16[2048,3584]{1,0:T(8,128)(2,1)} %all-gather.12.cloned.1.call-done, bf16[512,3584]{1,0:T(8,128)(2,1)} %param.7), kind=kOutput, calls=%fused_computation.7 | convolution fusion | flops 7517241344 | bytes 26738688 | tf_op jit(solution)/shard_map/nf,df->nd/dot_general | solution.py:48
  938.3 13.6 %fusion.10 = f32[3584,512]{1,0:T(8,128)} fusion(bf16[2048,3584]{1,0:T(8,128)(2,1)} %all-gather.8.cloned.1.call-done, bf16[2048,512]{1,0:T(8,128)(2,1)} %bitcast.88), kind=kOutput, calls=%fused_computation.21 | convolution fusion | flops 7516192768 | bytes 24117248 | tf_op jit(solution)/shard_map/nf,nd->fd/dot_general | solution.py:39
  951.9 276.1 %all-reduce.5.cloned.1.call-done = (f32[8,4,64,512]{3,2,1,0:T(8,128)}, f32[8,4,64,512]{3,2,1,0:T(8,128)}) async-done(((f32[8,4,64,512]{3,2,1,0:T(8,128)}, f32[8,4,64,512]{3,2,1,0:T(8,128)}), (f32[8,4,64,512]{3,2,1,0:T(8,128)}, f32[8,4,64,512]{3,2,1,0:T(8,128)})) %all-reduce.5.cloned.1.call-update) | async-done | bytes 8388624
  1228.0 2.9 fusion.2
  1230.9 3.7 all-to-all-start.3
  1234.6 13.0 %convolution_bitcast_fusion.1 = f32[512,3584]{0,1:T(8,128)} fusion(bf16[2048,3584]{1,0:T(8,128)(2,1)} %all-gather.10.cloned.1.call-done, bf16[2048,512]{1,0:T(8,128)(2,1)S(1)} %bitcast.85), kind=kOutput, calls=%fused_computation.1 | convolution fusion | flops 7516192768 | bytes 24117248 | tf_op jit(solution)/shard_map/nd,nf->df/dot_general | solution.py:45
  1247.6 2.9 fusion.4
  1250.5 4.1 all-to-all-start.1
  1254.6 13.0 %convolution_bitcast_fusion = f32[512,3584]{0,1:T(8,128)} fusion(bf16[2048,3584]{1,0:T(8,128)(2,1)} %all-gather.12.cloned.1.call-done, bf16[2048,512]{1,0:T(8,128)(2,1)S(1)} %bitcast.86), kind=kOutput, calls=%fused_computation | convolution fusion | flops 7516192768 | bytes 24117248 | tf_op jit(solution)/shard_map/nd,nf->df/dot_general | solution.py:46
  1267.6 8.4 copy.36
  1275.9 8.4 copy.37
  (38 shorter events, 7.2 us)
Async XLA Ops:
  7.2 17.1 %copy-start.3 = (bf16[64,4096]{1,0:T(8,128)(2,1)S(1)}, bf16[64,4096]{1,0:T(8,128)(2,1)}, u32[]{:S(2)}) copy-start(bf16[64,4096]{1,0:T(8,128)(2,1)} %param.5) | copy-start | bytes 1572868
  7.2 62.2 %all-gather.16.cloned.1.call-start = ((), (), s32[]{:S(2)}) async-start(), calls=%async_computation.14 | async-start | bytes 2621440 | tf_op jit(solution)/shard_map/all_gather | solution.py:16
  24.2 91.8 %all-gather.14.cloned.1.call-start = ((), (), s32[]{:S(2)}) async-start(), calls=%async_computation.13 | async-start | bytes 2621440 | tf_op jit(solution)/shard_map/all_gather | solution.py:16
  36.4 0.8 copy-start
  38.3 261.1 %reduce-scatter.14.cloned.1.call-start = ((), (), s32[]{:S(2)}) async-start(), calls=%async_computation.10 | async-start | bytes 33030144 | tf_op jit(solution)/shard_map/reduce_scatter | solution.py:38
  69.3 3.7 copy-start.4
  71.8 1.3 copy-start.2
  86.9 397.0 %reduce-scatter.12.cloned.1.call-start = ((), (), s32[]{:S(2)}) async-start(), calls=%async_computation.8 | async-start | bytes 33030144 | tf_op jit(solution)/shard_map/reduce_scatter | solution.py:30
  116.0 2.7 copy-start.5
  138.3 530.1 %reduce-scatter.10.cloned.1.call-start = ((), (), s32[]{:S(2)}) async-start(), calls=%async_computation.7 | async-start | bytes 33030144 | tf_op jit(solution)/shard_map/reduce_scatter | solution.py:29
  160.2 596.1 %all-gather.8.cloned.1.call-start = ((), (), s32[]{:S(2)}) async-start(), calls=%async_computation.9 | async-start | bytes 16515072 | tf_op jit(solution)/shard_map/all_gather | solution.py:34
  675.2 164.4 %all-gather.10.cloned.1.call-start = ((), (), s32[]{:S(2)}) async-start(), calls=%async_computation.11 | async-start | bytes 16515072 | tf_op jit(solution)/shard_map/all_gather | solution.py:43
  676.0 247.0 %all-gather.12.cloned.1.call-start = ((), (), s32[]{:S(2)}) async-start(), calls=%async_computation.12 | async-start | bytes 16515072 | tf_op jit(solution)/shard_map/all_gather | solution.py:44
  676.7 551.3 %all-reduce.5.cloned.1.call-start = ((), (), s32[]{:S(2)}) async-start(), calls=%async_computation.15 | async-start | bytes 16777216
  937.0 0.7 copy-start.6
  1230.9 19.6 %all-to-all-start.3 = ((bf16[8,64,512]{2,1,0:T(8,128)(2,1)}), bf16[8,64,512]{2,1,0:T(8,128)(2,1)S(1)}, u32[]{:S(2)}, u32[]{:S(2)}) async-start(bf16[8,64,512]{2,1,0:T(8,128)(2,1)} %fusion.2), calls=%async_computation.6 | async-start | bytes 1048576 | tf_op jit(solution)/shard_map/all_to_all | solution.py:24
  1234.6 13.0 %copy-start.1 = (bf16[64,8,512]{2,0,1:T(8,128)(2,1)S(1)}, bf16[64,8,512]{2,0,1:T(8,128)(2,1)}, u32[]{:S(2)}) copy-start(bf16[64,8,512]{2,0,1:T(8,128)(2,1)} %copy-done) | copy-start | bytes 1572868
  1250.5 34.7 %all-to-all-start.1 = ((bf16[8,64,512]{2,1,0:T(8,128)(2,1)}), bf16[8,64,512]{2,1,0:T(8,128)(2,1)S(1)}, u32[]{:S(2)}, u32[]{:S(2)}) async-start(bf16[8,64,512]{2,1,0:T(8,128)(2,1)} %fusion.4), calls=%async_computation.3 | async-start | bytes 1048576 | tf_op jit(solution)/shard_map/all_to_all | solution.py:24
Sparse Core Ops, SparseCore 0:
  24.3 45.0 all-gather.15
  71.5 44.4 all-gather.13
  119.6 179.7 reduce-scatter.13
  302.9 180.9 reduce-scatter.11
  487.4 180.9 reduce-scatter.9
  675.3 80.8 all-gather.7
  758.7 80.8 all-gather.9
  842.0 80.8 all-gather.11
  937.1 290.8 all-reduce.4
where the time goes:
time: 1290 us
  waiting for transfers between devices  1070 us (83%)
  matrix products  135 us (10%)
  local copies, waits for them, and re-layouts  30.2 us (2%)
  blocking collectives  26.8 us (2%)
  between operations  13.9 us (1%)
    unnamed x10, waiting for transfers between devices  278 us
    reduce_scatter x1, waiting for transfers between devices, local_step(): lax.psum_scatter(jnp.dot(x_cols, wu_loc, preferred_element_type=jnp.float...  184 us
    reduce_scatter x1, waiting for transfers between devices, local_step(): lax.psum_scatter(jnp.dot(x_cols, wg_loc, preferred_element_type=jnp.float...  184 us
    reduce_scatter x1, waiting for transfers between devices, local_step(): lax.psum_scatter(jnp.einsum('nd,fd->nf', gy_cols, wd_loc, preferred_eleme...  139 us
    all_gather x1, waiting for transfers between devices, local_step(): hidden_all = lax.all_gather(hidden, 'dp', axis=0, tiled=True)  79.5 us
    all_gather x1, waiting for transfers between devices, local_step(): gate_all = lax.all_gather(grad_gate, 'dp', axis=0, tiled=True)  70 us
    all_gather x1, waiting for transfers between devices, local_step(): up_all = lax.all_gather(grad_up, 'dp', axis=0, tiled=True)  70 us
    all_gather x2, waiting for transfers between devices, spread_cols(): gathered = lax.all_gather(cols_mine, 'tp', axis=1)  60 us
  transfers between devices with their start and end apart: 11, of which 9 were waited for; matrix products, arithmetic and copies ran while one was open for 11% of the time, Pallas kernels for 0%

commit v1 on v0

v1 whole, which is shorter than its diff:
```python
import jax
import jax.numpy as jnp
from jax import lax
from jax.sharding import PartitionSpec as P


def solution(mesh):
    dp_size = mesh.shape["dp"]
    tp_size = mesh.shape["tp"]
    flip = {o: [(i, i ^ o) for i in range(dp_size)] for o in (1, 2, 4, 6)}
    bf16, f32 = jnp.bfloat16, jnp.float32

    def swap(v, o):
        return lax.ppermute(v, "dp", flip[o])

    def local_step(x_loc, wg_loc, wu_loc, wd_loc, gy_loc):
        me = lax.axis_index("dp")
        tz = lax.axis_index("tp")
        core = me % 2
        chip = me // 2
        tok, d_model = x_loc.shape
        d_loc, ff_loc = wg_loc.shape
        fq = ff_loc // 4
        half = 2 * tp_size * tok
        n_own = 2 * half

        def split_full(full):
            full = full.reshape(tp_size, 2, 2, 2, tok, d_model)
            rows = lax.dynamic_index_in_dim(full, core, 3, keepdims=False).reshape(n_own, d_model)
            cols = []
            for i in range(2):
                c = lax.dynamic_slice(full, (0, 0, 0, (core + i) % 2, 0, me * d_loc),
                                      (tp_size, 2, 2, 1, tok, d_loc))
                cols.append(c.reshape(tp_size, 2, 2 * tok, d_loc).transpose(1, 0, 2, 3))
            return rows, cols

        def quarter(w, f_axis, o):
            return lax.dynamic_slice_in_dim(w, (chip ^ (o // 2)) * fq, fq, f_axis)

        def exchange(piece):
            got = {0: piece(0)}
            for o in (2, 4, 6):
                got[o] = swap(piece(o), o)
            return got

        def place(axis, *gots):
            width, rows = gots[0][0].shape[axis], gots[0][0].shape[0]
            shape = list(gots[0][0].shape)
            shape[axis] = 4 * width
            shape[0] *= len(gots)
            out = jnp.zeros(shape, bf16)
            for o in (0, 2, 4, 6):
                for i, got in enumerate(gots):
                    start = [i * rows, 0]
                    start[axis] += (chip ^ (o // 2)) * width
                    out = lax.dynamic_update_slice(out, got[o], tuple(start))
            return out

        def near(a, b):
            return {0: a, 2: swap(a, 2), 4: swap(a, 4)}, {0: b, 4: swap(b, 4), 2: swap(b, 2)}

        def far(got_a, got_b):
            return {**got_a, 6: swap(got_a[2], 4)}, {**got_b, 6: swap(got_b[4], 2)}

        def send_z(parts):
            def blk(o):
                return jnp.stack([lax.dynamic_index_in_dim(p, (tz + o) % tp_size, 1, keepdims=False) for p in parts])

            got = [blk(0)]
            for o in (2, 1, 3):
                perm = [(i, (i + o) % tp_size) for i in range(tp_size)]
                got.append(lax.ppermute(blk(o), "tp", perm))
            return got

        def finish(total, cols):
            resid = jnp.stack([lax.dynamic_index_in_dim(c, tz, 1, keepdims=False) for c in cols])
            s = (total + resid.astype(f32)).astype(bf16)
            s = jnp.where(core == 0, s, jnp.flip(s, axis=0))
            s = s.reshape(2, 4, tok, d_loc).transpose(1, 0, 2, 3).reshape(dp_size, tok, d_loc)
            s = lax.all_to_all(s, "dp", 0, 2, tiled=True)
            return s.reshape(tok, d_model)

        def dot2(rows, ws, eq):
            return (jnp.einsum(eq, rows[0], ws[0], preferred_element_type=f32)
                    + jnp.einsum(eq, rows[1], ws[1], preferred_element_type=f32))

        x_full = lax.all_gather(x_loc, ("tp", "dp"), axis=0, tiled=True)
        gy_full = lax.all_gather(gy_loc, ("tp", "dp"), axis=0, tiled=True)
        got_gu = exchange(lambda o: jnp.concatenate([quarter(wg_loc, 1, o), quarter(wu_loc, 1, o)], axis=1))
        wd_late, got_gu[2], got_gu[4] = lax.optimization_barrier((wd_loc, got_gu[2], got_gu[4]))
        got_d = exchange(lambda o: quarter(wd_late, 0, o))

        wgu = place(0, got_gu)
        wgu = (wgu.reshape(4, d_loc, 2 * fq), swap(wgu, 1).reshape(4, d_loc, 2 * fq))
        wgu = jnp.where(core == 0, jnp.stack(wgu, axis=1), jnp.stack(wgu[::-1], axis=1)).reshape(d_model, 2 * fq)
        x_full, got_d[2], got_d[4], got_d[6] = lax.optimization_barrier((x_full, got_d[2], got_d[4], got_d[6]))
        x_rows, x_cols = split_full(x_full)
        wd_all = place(1, got_d)
        wd_pair = (wd_all, swap(wd_all, 1))
        wd_all = jnp.zeros((fq, d_model), bf16)
        for i in range(2):
            for c in range(4):
                wd_all = lax.dynamic_update_slice(wd_all, wd_pair[i][:, c * d_loc:(c + 1) * d_loc],
                                                  (0, (2 * c + (core + i) % 2) * d_loc))
        pre = jnp.dot(x_rows, wgu, preferred_element_type=f32)
        gate_pre, up_pre = pre[:, :fq], pre[:, fq:]
        sig = jax.nn.sigmoid(gate_pre)
        silu = gate_pre * sig
        hidden = (silu * up_pre).astype(bf16).reshape(tp_size, 2, 2 * tok, fq)
        got_h = far(*near(hidden[:, 0].reshape(half, fq), hidden[:, 1].reshape(half, fq)))
        h_own = place(1, *got_h)

        h_all = (h_own, swap(h_own, 1))
        y_part = [jnp.dot(h, wd_loc, preferred_element_type=f32) for h in h_all]
        gy_full, _ = lax.optimization_barrier((gy_full, y_part))
        y_got = send_z([p.reshape(2, tp_size, 2 * tok, d_loc) for p in y_part])
        gy_rows, gy_cols = split_full(gy_full)
        grad_h = jnp.einsum("nd,fd->nf", gy_rows, wd_all, preferred_element_type=f32)
        deriv = sig * (1.0 + gate_pre * (1.0 - sig))
        d_gate = (grad_h * up_pre * deriv).astype(bf16).reshape(tp_size, 2, 2 * tok, fq)
        d_up = (grad_h * silu).astype(bf16).reshape(tp_size, 2, 2 * tok, fq)
        got_0 = near(d_gate[:, 0].reshape(half, fq), d_up[:, 0].reshape(half, fq))
        got_1 = near(d_gate[:, 1].reshape(half, fq), d_up[:, 1].reshape(half, fq))
        got_0, got_1 = far(*got_0), far(*got_1)
        grad_wd = dot2(h_all, [c.reshape(n_own, d_loc) for c in gy_cols], "nf,nd->fd")

        grad_wg = grad_wu = None
        x_got = []
        for y in range(2):
            got = (got_0, got_1)[y]
            dg, du = place(1, got[0]), place(1, got[1])
            dg, du = (dg, swap(dg, 1)), (du, swap(du, 1))
            part = [jnp.einsum("nf,df->nd", dg[i], wg_loc, preferred_element_type=f32)
                    + jnp.einsum("nf,df->nd", du[i], wu_loc, preferred_element_type=f32) for i in range(2)]
            x_got.append(send_z([p.reshape(1, tp_size, 2 * tok, d_loc) for p in part]))
            xc = [c[y].reshape(half, d_loc) for c in x_cols]
            part_g = dot2(xc, dg, "nd,nf->df")
            part_u = dot2(xc, du, "nd,nf->df")
            grad_wg = part_g if grad_wg is None else grad_wg + part_g
            grad_wu = part_u if grad_wu is None else grad_wu + part_u
        y_rows = finish(sum(y_got[1:], y_got[0]), x_cols)
        x_got = [sum(g[1:], g[0]) for g in x_got]
        gx_rows = finish(jnp.concatenate(x_got, axis=1), gy_cols)
        return y_rows, gx_rows, grad_wg, grad_wu, grad_wd


    row_spec = P(("dp", "tp"), None)
    up_spec = P("dp", "tp")
    down_spec = P("tp", "dp")
    return jax.shard_map(local_step, mesh=mesh,
                         in_specs=(row_spec, up_spec, up_spec, down_spec, row_spec),
                         out_specs=(row_spec, row_spec, up_spec, up_spec, down_spec),
                         check_vma=False)
```

time: 1290 us -> 696 us (0.54)
  waiting for transfers between devices: 1070 us -> 346 us
  local copies, waits for them, and re-layouts: 30.2 us -> 117 us
  starting transfers between devices: 8.38 us -> 49.6 us
  blocking collectives: 26.8 us -> 0 us
  other arithmetic: 12.5 us -> 32.7 us
    reduce_scatter x3 -> x0, waiting for transfers between devices: 508 us -> none  [the longest x1 184 us: local_step(): lax.psum_scatter(jnp.dot(x_cols, wu_loc, preferred_element_type=jnp.float...]
    ppermute x0 -> x40, waiting for transfers between devices: none -> 315 us  [the longest x31 237 us: swap(): return lax.ppermute(v, 'dp', flip[o])]
    all_gather x5 -> x2, waiting for transfers between devices: 279 us -> 0.01 us  [the longest x1 0.01 us: local_step(): x_full = lax.all_gather(x_loc, ('tp', 'dp'), axis=0, tiled=True)]
    unnamed x10 -> x2, waiting for transfers between devices: 278 us -> 1.38 us
    dynamic_update_slice x0 -> x39, local copies, waits for them, and re-layouts: none -> 60.2 us  [the longest x31 42.8 us: place(): out = lax.dynamic_update_slice(out, got[o], tuple(start))]
    ppermute x0 -> x40, starting transfers between devices: none -> 42.1 us  [the longest x31 28.6 us: swap(): return lax.ppermute(v, 'dp', flip[o])]
    all_to_all x2, waiting for transfers between devices: 0.01 us -> 29.4 us  [finish(): s = lax.all_to_all(s, 'dp', 0, 2, tiled=True)]
    all_to_all x2 -> x0, blocking collectives: 26.8 us -> none  [spread_cols(): cols_mine = lax.all_to_all(rows_loc, 'dp', 1, 0, tiled=True)]
  transfers between devices with their start and end apart: 11 -> 44, of which waited for: 9 -> 17; matrix products, arithmetic and copies ran while one was open for 11% -> 36% of each run, Pallas kernels for 0% -> 0%
where the time goes in v1:
time: 696 us; the launch traced here: 692 us
  waiting for transfers between devices  346 us (50%)
  matrix products  132 us (19%)
  local copies, waits for them, and re-layouts  117 us (17%)
  starting transfers between devices  49.6 us (7%)
  other arithmetic  32.7 us (5%)
  between operations  15.1 us (2%)
    ppermute x31, waiting for transfers between devices, swap(): return lax.ppermute(v, 'dp', flip[o])  237 us
    ppermute x9, waiting for transfers between devices, send_z(): got.append(lax.ppermute(blk(o), 'tp', perm))  78.1 us
    dynamic_update_slice x31, local copies, waits for them, and re-layouts, place(): out = lax.dynamic_update_slice(out, got[o], tuple(start))  42.8 us
    dot_general x5, matrix products, dot2(): jnp.einsum(eq, rows[0], ws[0], preferred_element_type=f32)  38.7 us
    all_to_all x2, waiting for transfers between devices, finish(): s = lax.all_to_all(s, 'dp', 0, 2, tiled=True)  29.4 us
    ppermute x31, starting transfers between devices, swap(): return lax.ppermute(v, 'dp', flip[o])  28.6 us
    dot_general x5, matrix products, dot2(): jnp.einsum(eq, rows[1], ws[1], preferred_element_type=f32)  23.1 us
    dot_general x1, matrix products, local_step(): pre = jnp.dot(x_rows, wgu, preferred_element_type=f32)  19 us
  transfers between devices with their start and end apart: 44, of which 17 were waited for; matrix products, arithmetic and copies ran while one was open for 36% of the time, Pallas kernels for 0%

profile of v1, /device:TPU:0, one launch (start us, length us, event | category | flops | bytes accessed | tf_op | source)
XLA Modules:
  0.0 691.9 jit_solution(18121003136590225003)
XLA Ops:
  26.0 50.3 %collective-permute-done = bf16[512,1792]{1,0:T(8,128)(2,1)} collective-permute-done((bf16[512,1792]{1,0:T(8,128)(2,1)}, bf16[512,1792]{1,0:T(8,128)(2,1)}, u32[]{:S(2)}, u32[]{:S(2)}) %collective-permute-start) | collective-permute-done | bytes 1835040 | tf_op jit(solution)/shard_map/ppermute | solution.py:14
  82.0 56.0 %collective-permute-done.5 = bf16[512,1792]{1,0:T(8,128)(2,1)} collective-permute-done((bf16[512,1792]{1,0:T(8,128)(2,1)}, bf16[512,1792]{1,0:T(8,128)(2,1)}, u32[]{:S(2)}, u32[]{:S(2)}) %collective-permute-start.5) | collective-permute-done | bytes 1835040 | tf_op jit(solution)/shard_map/ppermute | solution.py:14
  149.4 4.6 collective-permute-done.6
  154.0 17.6 %maximum_select_fusion = bf16[4,2,512,1792]{3,2,1,0:T(8,128)(2,1)} fusion(bf16[4,1,512,1792]{3,2,1,0:T(8,128)(2,1)} %bitcast.3, bf16[4,1,512,1792]{3,2,1,0:T(8,128)(2,1)} %bitcast.2, pred[]{:T(512)S(6)} %eq.43), kind=kLoop, calls=%fused_computation | loop fusion | flops 22020096 | bytes 29360128 | tf_op jit(solution)/shard_map/jit(_where)/select_n | solution.py:95
  171.6 16.0 %collective-permute-done.3 = bf16[896,512]{1,0:T(8,128)(2,1)S(1)} collective-permute-done((bf16[896,512]{1,0:T(8,128)(2,1)S(1)}, bf16[896,512]{1,0:T(8,128)(2,1)S(1)}, u32[]{:S(2)}, u32[]{:S(2)}) %collective-permute-start.3) | collective-permute-done | bytes 917536 | tf_op jit(solution)/shard_map/ppermute | solution.py:14
  187.6 5.0 collective-permute-done.4
  192.6 7.8 %constant_dynamic-slice_fusion.29 = bf16[4,2,2,1,64,4096]{5,4,3,2,1,0:T(8,128)(2,1)} fusion(bf16[4,2,2,2,64,4096]{5,4,3,2,1,0:T(8,128)(2,1)} %bitcast.142, s32[]{:T(128)S(6)} %select_n.275), kind=kLoop, calls=%fused_computation.113 | loop fusion | bytes 16777220 | tf_op jit(solution)/shard_map/jit(dynamic_index_in_dim)/dynamic_slice | solution.py:29
  200.4 19.0 %fusion.15 = f32[1024,1792]{1,0:T(8,128)S(1)} fusion(bf16[1024,4096]{1,0:T(8,128)(2,1)} %bitcast.138, bf16[4096,1792]{1,0:T(8,128)(2,1)} %bitcast.136), kind=kOutput, calls=%fused_computation.130 | convolution fusion | flops 15032385536 | bytes 30408704 | tf_op jit(solution)/shard_map/dot_general | solution.py:105
  226.7 24.5 %collective-permute-done.7 = bf16[512,896]{1,0:T(8,128)(2,1)S(1)} collective-permute-done((bf16[512,896]{1,0:T(8,128)(2,1)S(1)}, bf16[512,896]{1,0:T(8,128)(2,1)S(1)}, u32[]{:S(2)}, u32[]{:S(2)}) %collective-permute-start.7) | collective-permute-done | bytes 917536 | tf_op jit(solution)/shard_map/ppermute | solution.py:14
  261.0 29.5 %collective-permute-done.8 = bf16[512,896]{1,0:T(8,128)(2,1)S(1)} collective-permute-done((bf16[512,896]{1,0:T(8,128)(2,1)S(1)}, bf16[512,896]{1,0:T(8,128)(2,1)S(1)}, u32[]{:S(2)}, u32[]{:S(2)}) %collective-permute-start.8) | collective-permute-done | bytes 917536 | tf_op jit(solution)/shard_map/ppermute | solution.py:14
  295.3 19.8 %collective-permute-done.11 = bf16[512,896]{1,0:T(8,128)(2,1)S(1)} collective-permute-done((bf16[512,896]{1,0:T(8,128)(2,1)S(1)}, bf16[512,896]{1,0:T(8,128)(2,1)S(1)}, u32[]{:S(2)}, u32[]{:S(2)}) %collective-permute-start.11) | collective-permute-done | bytes 917536 | tf_op jit(solution)/shard_map/ppermute | solution.py:14
  325.0 4.0 broadcast_in_dim.14
  337.8 6.2 fusion.16
  353.8 7.5 %fusion.17 = f32[1024,512]{1,0:T(8,128)} fusion(bf16[1024,3584]{1,0:T(8,128)(2,1)} %collective-permute-done.13, bf16[3584,512]{1,0:T(8,128)(2,1)S(1)} %copy-done.11), kind=kOutput, calls=%fused_computation.132 | convolution fusion | flops 3758096384 | bytes 13107200 | tf_op jit(solution)/shard_map/dot_general | solution.py:114
  361.3 7.8 %constant_dynamic-slice_fusion.20 = bf16[4,2,2,1,64,4096]{5,4,3,2,1,0:T(8,128)(2,1)} fusion(bf16[4,2,2,2,64,4096]{5,4,3,2,1,0:T(8,128)(2,1)} %bitcast.140, s32[]{:T(128)S(6)} %select_n.275), kind=kLoop, calls=%fused_computation.97 | loop fusion | bytes 16777220 | tf_op jit(solution)/shard_map/jit(dynamic_index_in_dim)/dynamic_slice | solution.py:29
  369.2 16.4 %multiply_convert_fusion.1 = (bf16[1024,896]{1,0:T(8,128)(2,1)S(1)}, bf16[1024,896]{1,0:T(8,128)(2,1)S(1)}) fusion(f32[1024,1792]{1,0:T(8,128)} %copy-done.6, bf16[1024,4096]{1,0:T(8,128)(2,1)} %bitcast.137, bf16[896,4096]{1,0:T(8,128)(2,1)} %slice_dynamic-update-slice_fusion), kind=kOutput, calls=%fused_computation.5 | convolution fusion | flops 7528120320 | bytes 26738688 | tf_op jit(solution)/shard_map/nd,fd->nf/dot_general | solution.py:118
  396.3 6.3 fusion.28
  402.6 9.5 %convolution_add_fusion = f32[3584,512]{1,0:T(8,128)} fusion(f32[3584,512]{1,0:T(8,128)S(1)} %fusion.28, bf16[1024,3584]{1,0:T(8,128)(2,1)} %constant_dynamic-update-slice_fusion.26, bf16[1024,512]{1,0:T(8,128)(2,1)S(1)} %bitcast.191), kind=kOutput, calls=%fused_computation.3 | convolution fusion | flops 3759931392 | bytes 23068672 | tf_op jit(solution)/shard_map/nf,nd->fd/dot_general | solution.py:84
  418.2 10.6 %collective-permute-done.29 = bf16[512,896]{1,0:T(8,128)(2,1)} collective-permute-done((bf16[512,896]{1,0:T(8,128)(2,1)S(1)}, bf16[512,896]{1,0:T(8,128)(2,1)}, u32[]{:S(2)}, u32[]{:S(2)}) %collective-permute-start.29) | collective-permute-done | bytes 917536 | tf_op jit(solution)/shard_map/ppermute | solution.py:14
  430.3 17.1 %collective-permute-done.21 = bf16[512,896]{1,0:T(8,128)(2,1)S(1)} collective-permute-done((bf16[512,896]{1,0:T(8,128)(2,1)S(1)}, bf16[512,896]{1,0:T(8,128)(2,1)S(1)}, u32[]{:S(2)}, u32[]{:S(2)}) %collective-permute-start.21) | collective-permute-done | bytes 917536 | tf_op jit(solution)/shard_map/ppermute | solution.py:14
  455.6 29.7 %collective-permute-done.14 = f32[2,2,128,512]{3,2,1,0:T(8,128)S(1)} collective-permute-done((f32[2,2,128,512]{3,2,1,0:T(8,128)S(1)}, f32[2,2,128,512]{3,2,1,0:T(8,128)S(1)}, u32[]{:S(2)}, u32[]{:S(2)}) %collective-permute-start.14) | collective-permute-done | bytes 1048608 | tf_op jit(solution)/shard_map/ppermute | solution.py:72
  503.1 29.4 %all-to-all-done = bf16[8,64,512]{2,1,0:T(8,128)(2,1)S(1)} async-done(((bf16[8,64,512]{2,1,0:T(8,128)(2,1)}), bf16[8,64,512]{2,1,0:T(8,128)(2,1)S(1)}, u32[]{:S(2)}, u32[]{:S(2)}) %all-to-all-start) | async-done | bytes 524320 | tf_op jit(solution)/shard_map/all_to_all | solution.py:80
  542.7 4.3 fusion.20
  549.2 4.1 convolution_add_fusion.2
  559.2 5.1 fusion.25
  591.5 8.1 %add_add_fusion.1 = f32[512,3584]{1,0:T(8,128)} fusion(f32[512,3584]{1,0:T(8,128)S(1)} %fusion.24, f32[512,3584]{1,0:T(8,128)S(1)} %fusion.22, f32[512,3584]{1,0:T(8,128)S(1)} %fusion.23, bf16[512,512]{1,0:T(8,128)(2,1)S(1)} %bitcast.152, bf16[512,3584]{1,0:T(8,128)(2,1)} %constant_dynamic-update-slice_fusion.4), kind=kOutput, calls=%fused_computation.2 | convolution fusion | flops 1884553216 | bytes 33554432 | tf_op jit(solution)/shard_map/nd,nf->df/dot_general | solution.py:84
  599.6 7.5 %fusion.27 = f32[512,3584]{1,0:T(8,128)} fusion(bf16[512,512]{1,0:T(8,128)(2,1)} %bitcast.157, bf16[512,3584]{1,0:T(8,128)(2,1)} %copy-done.12), kind=kOutput, calls=%fused_computation.142 | convolution fusion | flops 1879048192 | bytes 11534336 | tf_op jit(solution)/shard_map/nd,nf->df/dot_general | solution.py:85
  608.7 5.0 fusion.26
  613.8 6.0 collective-permute-done.37
  621.4 11.0 %collective-permute-done.27 = f32[2,1,128,512]{3,2,1,0:T(8,128)} collective-permute-done((f32[2,1,128,512]{3,2,1,0:T(8,128)}, f32[2,1,128,512]{3,2,1,0:T(8,128)}, u32[]{:S(2)}, u32[]{:S(2)}) %collective-permute-start.27) | collective-permute-done | bytes 524320 | tf_op jit(solution)/shard_map/ppermute | solution.py:72
  632.4 31.4 %collective-permute-done.26 = f32[2,1,128,512]{3,2,1,0:T(8,128)S(1)} collective-permute-done((f32[2,1,128,512]{3,2,1,0:T(8,128)S(1)}, f32[2,1,128,512]{3,2,1,0:T(8,128)S(1)}, u32[]{:S(2)}, u32[]{:S(2)}) %collective-permute-start.26) | collective-permute-done | bytes 524320 | tf_op jit(solution)/shard_map/ppermute | solution.py:72
  670.0 13.9 %add_add_fusion = f32[512,3584]{1,0:T(8,128)} fusion(f32[512,3584]{1,0:T(8,128)} %fusion.27, f32[512,3584]{1,0:T(8,128)} %fusion.25, f32[512,3584]{1,0:T(8,128)} %fusion.26, bf16[512,512]{1,0:T(8,128)(2,1)S(1)} %bitcast.153, bf16[512,3584]{1,0:T(8,128)(2,1)} %constant_dynamic-update-slice_fusion), kind=kOutput, calls=%fused_computation.1 | convolution fusion | flops 1884553216 | bytes 33554432 | tf_op jit(solution)/shard_map/nd,nf->df/dot_general | solution.py:84
  (248 shorter events, 185.7 us)
Async XLA Ops:
  7.2 185.4 %all-gather.3.cloned.1.call-start = ((), (), s32[]{:S(2)}) async-start(), calls=%async_computation.2 | async-start | bytes 17301504 | tf_op jit(solution)/shard_map/all_gather | solution.py:87
  7.9 353.4 %all-gather.5.cloned.1.call-start = ((), (), s32[]{:S(2)}) async-start(), calls=%async_computation.3 | async-start | bytes 17301504 | tf_op jit(solution)/shard_map/all_gather | solution.py:88
  13.9 62.4 %collective-permute-start = (bf16[512,1792]{1,0:T(8,128)(2,1)}, bf16[512,1792]{1,0:T(8,128)(2,1)}, u32[]{:S(2)}, u32[]{:S(2)}) collective-permute-start(bf16[512,1792]{1,0:T(8,128)(2,1)} %pad_maximum_fusion), channel_id=1, source_target_pairs={{0,2},{1,3},{2,0},{3,1},{4,6},{5,7},{6,4},{7,5},{8,10},{9,11},{10,... | collective-permute-start | bytes 5505032 | tf_op jit(solution)/shard_map/ppermute | solution.py:14
  18.3 58.0 %collective-permute-start.1 = (bf16[512,1792]{1,0:T(8,128)(2,1)}, bf16[512,1792]{1,0:T(8,128)(2,1)}, u32[]{:S(2)}, u32[]{:S(2)}) collective-permute-start(bf16[512,1792]{1,0:T(8,128)(2,1)} %pad_maximum_fusion.1), channel_id=1, source_target_pairs={{0,4},{1,5},{2,6},{3,7},{4,0},{5,1},{6,2},{7,3},{8,12},{9,13},{10,... | collective-permute-start | bytes 5505032 | tf_op jit(solution)/shard_map/ppermute | solution.py:14
  21.2 116.9 %collective-permute-start.5 = (bf16[512,1792]{1,0:T(8,128)(2,1)}, bf16[512,1792]{1,0:T(8,128)(2,1)}, u32[]{:S(2)}, u32[]{:S(2)}) collective-permute-start(bf16[512,1792]{1,0:T(8,128)(2,1)} %pad_maximum_fusion.2), channel_id=1, source_target_pairs={{0,6},{1,7},{2,4},{3,5},{4,2},{5,3},{6,0},{7,1},{8,14},{9,15},{10,... | collective-permute-start | bytes 5505032 | tf_op jit(solution)/shard_map/ppermute | solution.py:14
  147.9 39.7 %collective-permute-start.3 = (bf16[896,512]{1,0:T(8,128)(2,1)S(1)}, bf16[896,512]{1,0:T(8,128)(2,1)S(1)}, u32[]{:S(2)}, u32[]{:S(2)}) collective-permute-start(bf16[896,512]{1,0:T(8,128)(2,1)S(1)} %get-tuple-element.29), channel_id=1, source_target_pairs={{0,4},{1,5},{2,6},{3,7},{4,0},{5,1},{6,2},{7,3},{8,12},{9,13},{10,... | collective-permute-start | bytes 2752520 | tf_op jit(solution)/shard_map/ppermute | solution.py:14
  148.7 43.9 %collective-permute-start.4 = (bf16[896,512]{1,0:T(8,128)(2,1)S(1)}, bf16[896,512]{1,0:T(8,128)(2,1)S(1)}, u32[]{:S(2)}, u32[]{:S(2)}) collective-permute-start(bf16[896,512]{1,0:T(8,128)(2,1)S(1)} %get-tuple-element.28), channel_id=1, source_target_pairs={{0,6},{1,7},{2,4},{3,5},{4,2},{5,3},{6,0},{7,1},{8,14},{9,15},{10,... | collective-permute-start | bytes 2752520 | tf_op jit(solution)/shard_map/ppermute | solution.py:14
  225.6 64.9 %collective-permute-start.8 = (bf16[512,896]{1,0:T(8,128)(2,1)S(1)}, bf16[512,896]{1,0:T(8,128)(2,1)S(1)}, u32[]{:S(2)}, u32[]{:S(2)}) collective-permute-start(bf16[512,896]{1,0:T(8,128)(2,1)S(1)} %bitcast.176), channel_id=1, source_target_pairs={{0,2},{1,3},{2,0},{3,1},{4,6},{5,7},{6,4},{7,5},{8,10},{9,11},{10,... | collective-permute-start | bytes 2752520 | tf_op jit(solution)/shard_map/ppermute | solution.py:14
  226.0 67.3 %collective-permute-start.9 = (bf16[512,896]{1,0:T(8,128)(2,1)S(1)}, bf16[512,896]{1,0:T(8,128)(2,1)S(1)}, u32[]{:S(2)}, u32[]{:S(2)}) collective-permute-start(bf16[512,896]{1,0:T(8,128)(2,1)S(1)} %bitcast.173), channel_id=1, source_target_pairs={{0,4},{1,5},{2,6},{3,7},{4,0},{5,1},{6,2},{7,3},{8,12},{9,13},{10,... | collective-permute-start | bytes 2752520 | tf_op jit(solution)/shard_map/ppermute | solution.py:14
  251.2 63.9 %collective-permute-start.11 = (bf16[512,896]{1,0:T(8,128)(2,1)S(1)}, bf16[512,896]{1,0:T(8,128)(2,1)S(1)}, u32[]{:S(2)}, u32[]{:S(2)}) collective-permute-start(bf16[512,896]{1,0:T(8,128)(2,1)S(1)} %collective-permute-done.7), channel_id=1, source_target_pairs={{0,4},{1,5},{2,6},{3,7},{4,0},{5,1},{6,2},{7,3},{8,12},{9,13},{10,... | collective-permute-start | bytes 2752520 | tf_op jit(solution)/shard_map/ppermute | solution.py:14
  253.9 62.2 %collective-permute-start.12 = (bf16[512,896]{1,0:T(8,128)(2,1)S(1)}, bf16[512,896]{1,0:T(8,128)(2,1)S(1)}, u32[]{:S(2)}, u32[]{:S(2)}) collective-permute-start(bf16[512,896]{1,0:T(8,128)(2,1)S(1)} %collective-permute-done.10), channel_id=1, source_target_pairs={{0,2},{1,3},{2,0},{3,1},{4,6},{5,7},{6,4},{7,5},{8,10},{9,11},{10,... | collective-permute-start | bytes 2752520 | tf_op jit(solution)/shard_map/ppermute | solution.py:14
  317.1 36.7 %collective-permute-start.13 = (bf16[1024,3584]{1,0:T(8,128)(2,1)}, bf16[1024,3584]{1,0:T(8,128)(2,1)}, u32[]{:S(2)}, u32[]{:S(2)}) collective-permute-start(bf16[1024,3584]{1,0:T(8,128)(2,1)} %constant_dynamic-update-slice_fusion.26), channel_id=1, source_target_pairs={{0,1},{1,0},{2,3},{3,2},{4,5},{5,4},{6,7},{7,6},{8,9},{9,8},{10,11... | collective-permute-start | bytes 22020104 | tf_op jit(solution)/shard_map/ppermute | solution.py:14
  389.9 59.7 %collective-permute-start.16 = (f32[2,2,128,512]{3,2,1,0:T(8,128)S(1)}, f32[2,2,128,512]{3,2,1,0:T(8,128)S(1)}, u32[]{:S(2)}, u32[]{:S(2)}) collective-permute-start(f32[2,2,128,512]{3,2,1,0:T(8,128)S(1)} %pad_maximum_fusion.5), channel_id=1, source_target_pairs={{0,24},{8,0},{16,8},{24,16},{1,25},{9,1},{17,9},{25,17},{2,26},{10... | collective-permute-start | bytes 3145736 | tf_op jit(solution)/shard_map/ppermute | solution.py:72
  395.4 52.0 %collective-permute-start.21 = (bf16[512,896]{1,0:T(8,128)(2,1)S(1)}, bf16[512,896]{1,0:T(8,128)(2,1)S(1)}, u32[]{:S(2)}, u32[]{:S(2)}) collective-permute-start(bf16[512,896]{1,0:T(8,128)(2,1)S(1)} %bitcast.160), channel_id=1, source_target_pairs={{0,2},{1,3},{2,0},{3,1},{4,6},{5,7},{6,4},{7,5},{8,10},{9,11},{10,... | collective-permute-start | bytes 2752520 | tf_op jit(solution)/shard_map/ppermute | solution.py:14
  415.7 39.0 %collective-permute-start.15 = (f32[2,2,128,512]{3,2,1,0:T(8,128)S(1)}, f32[2,2,128,512]{3,2,1,0:T(8,128)S(1)}, u32[]{:S(2)}, u32[]{:S(2)}) collective-permute-start(f32[2,2,128,512]{3,2,1,0:T(8,128)S(1)} %pad_maximum_fusion.4), channel_id=1, source_target_pairs={{0,8},{8,16},{16,24},{24,0},{1,9},{9,17},{17,25},{25,1},{2,10},{10... | collective-permute-start | bytes 3145736 | tf_op jit(solution)/shard_map/ppermute | solution.py:72
  415.8 69.6 %collective-permute-start.14 = (f32[2,2,128,512]{3,2,1,0:T(8,128)S(1)}, f32[2,2,128,512]{3,2,1,0:T(8,128)S(1)}, u32[]{:S(2)}, u32[]{:S(2)}) collective-permute-start(f32[2,2,128,512]{3,2,1,0:T(8,128)S(1)} %pad_maximum_fusion.3), channel_id=1, source_target_pairs={{0,16},{8,24},{16,0},{24,8},{1,17},{9,25},{17,1},{25,9},{2,18},{10... | collective-permute-start | bytes 3145736 | tf_op jit(solution)/shard_map/ppermute | solution.py:72
  428.8 58.5 %collective-permute-start.30 = (bf16[512,896]{1,0:T(8,128)(2,1)S(1)}, bf16[512,896]{1,0:T(8,128)(2,1)S(1)}, u32[]{:S(2)}, u32[]{:S(2)}) collective-permute-start(bf16[512,896]{1,0:T(8,128)(2,1)S(1)} %bitcast.168), channel_id=1, source_target_pairs={{0,4},{1,5},{2,6},{3,7},{4,0},{5,1},{6,2},{7,3},{8,12},{9,13},{10,... | collective-permute-start | bytes 2752520 | tf_op jit(solution)/shard_map/ppermute | solution.py:14
  447.4 40.5 %collective-permute-start.22 = (bf16[512,896]{1,0:T(8,128)(2,1)S(1)}, bf16[512,896]{1,0:T(8,128)(2,1)}, u32[]{:S(2)}, u32[]{:S(2)}) collective-permute-start(bf16[512,896]{1,0:T(8,128)(2,1)S(1)} %bitcast.162), channel_id=1, source_target_pairs={{0,4},{1,5},{2,6},{3,7},{4,0},{5,1},{6,2},{7,3},{8,12},{9,13},{10,... | collective-permute-start | bytes 2752520 | tf_op jit(solution)/shard_map/ppermute | solution.py:14
  449.7 43.6 %collective-permute-start.18 = (bf16[512,896]{1,0:T(8,128)(2,1)S(1)}, bf16[512,896]{1,0:T(8,128)(2,1)}, u32[]{:S(2)}, u32[]{:S(2)}) collective-permute-start(bf16[512,896]{1,0:T(8,128)(2,1)S(1)} %bitcast.164), channel_id=1, source_target_pairs={{0,2},{1,3},{2,0},{3,1},{4,6},{5,7},{6,4},{7,5},{8,10},{9,11},{10,... | collective-permute-start | bytes 2752520 | tf_op jit(solution)/shard_map/ppermute | solution.py:14
  454.7 46.1 %collective-permute-start.19 = (bf16[512,896]{1,0:T(8,128)(2,1)S(1)}, bf16[512,896]{1,0:T(8,128)(2,1)}, u32[]{:S(2)}, u32[]{:S(2)}) collective-permute-start(bf16[512,896]{1,0:T(8,128)(2,1)S(1)} %bitcast.165), channel_id=1, source_target_pairs={{0,4},{1,5},{2,6},{3,7},{4,0},{5,1},{6,2},{7,3},{8,12},{9,13},{10,... | collective-permute-start | bytes 2752520 | tf_op jit(solution)/shard_map/ppermute | solution.py:14
  485.4 47.9 %collective-permute-start.34 = (bf16[512,896]{1,0:T(8,128)(2,1)}, bf16[512,896]{1,0:T(8,128)(2,1)}, u32[]{:S(2)}, u32[]{:S(2)}) collective-permute-start(bf16[512,896]{1,0:T(8,128)(2,1)} %collective-permute-done.33), channel_id=1, source_target_pairs={{0,2},{1,3},{2,0},{3,1},{4,6},{5,7},{6,4},{7,5},{8,10},{9,11},{10,... | collective-permute-start | bytes 2752520 | tf_op jit(solution)/shard_map/ppermute | solution.py:14
  487.4 48.6 %collective-permute-start.31 = (bf16[512,896]{1,0:T(8,128)(2,1)}, bf16[512,896]{1,0:T(8,128)(2,1)}, u32[]{:S(2)}, u32[]{:S(2)}) collective-permute-start(bf16[512,896]{1,0:T(8,128)(2,1)} %collective-permute-done.29), channel_id=1, source_target_pairs={{0,4},{1,5},{2,6},{3,7},{4,0},{5,1},{6,2},{7,3},{8,12},{9,13},{10,... | collective-permute-start | bytes 2752520 | tf_op jit(solution)/shard_map/ppermute | solution.py:14
  487.9 50.7 %collective-permute-start.23 = (bf16[512,896]{1,0:T(8,128)(2,1)}, bf16[512,896]{1,0:T(8,128)(2,1)}, u32[]{:S(2)}, u32[]{:S(2)}) collective-permute-start(bf16[512,896]{1,0:T(8,128)(2,1)} %collective-permute-done.22), channel_id=1, source_target_pairs={{0,2},{1,3},{2,0},{3,1},{4,6},{5,7},{6,4},{7,5},{8,10},{9,11},{10,... | collective-permute-start | bytes 2752520 | tf_op jit(solution)/shard_map/ppermute | solution.py:14
  489.6 42.9 %all-to-all-start = ((bf16[8,64,512]{2,1,0:T(8,128)(2,1)}), bf16[8,64,512]{2,1,0:T(8,128)(2,1)S(1)}, u32[]{:S(2)}, u32[]{:S(2)}) async-start(bf16[8,64,512]{2,1,0:T(8,128)(2,1)} %bitcast.179), calls=%async_computation | async-start | bytes 1048576 | tf_op jit(solution)/shard_map/all_to_all | solution.py:80
  493.3 47.6 %collective-permute-start.20 = (bf16[512,896]{1,0:T(8,128)(2,1)}, bf16[512,896]{1,0:T(8,128)(2,1)}, u32[]{:S(2)}, u32[]{:S(2)}) collective-permute-start(bf16[512,896]{1,0:T(8,128)(2,1)} %collective-permute-done.18), channel_id=1, source_target_pairs={{0,4},{1,5},{2,6},{3,7},{4,0},{5,1},{6,2},{7,3},{8,12},{9,13},{10,... | collective-permute-start | bytes 2752520 | tf_op jit(solution)/shard_map/ppermute | solution.py:14
  540.8 35.7 %collective-permute-start.25 = (bf16[512,3584]{1,0:T(8,128)(2,1)}, bf16[512,3584]{1,0:T(8,128)(2,1)S(1)}, u32[]{:S(2)}, u32[]{:S(2)}) collective-permute-start(bf16[512,3584]{1,0:T(8,128)(2,1)} %constant_dynamic-update-slice_fusion.8), channel_id=1, source_target_pairs={{0,1},{1,0},{2,3},{3,2},{4,5},{5,4},{6,7},{7,6},{8,9},{9,8},{10,11... | collective-permute-start | bytes 11010056 | tf_op jit(solution)/shard_map/ppermute | solution.py:14
  542.3 36.3 %collective-permute-start.24 = (bf16[512,3584]{1,0:T(8,128)(2,1)S(1)}, bf16[512,3584]{1,0:T(8,128)(2,1)S(1)}, u32[]{:S(2)}, u32[]{:S(2)}) collective-permute-start(bf16[512,3584]{1,0:T(8,128)(2,1)S(1)} %constant_dynamic-update-slice_fusion.12), channel_id=1, source_target_pairs={{0,1},{1,0},{2,3},{3,2},{4,5},{5,4},{6,7},{7,6},{8,9},{9,8},{10,11... | collective-permute-start | bytes 11010056 | tf_op jit(solution)/shard_map/ppermute | solution.py:14
  575.1 38.7 %collective-permute-start.38 = (f32[2,1,128,512]{3,2,1,0:T(8,128)}, f32[2,1,128,512]{3,2,1,0:T(8,128)}, u32[]{:S(2)}, u32[]{:S(2)}) collective-permute-start(f32[2,1,128,512]{3,2,1,0:T(8,128)} %pad_maximum_fusion.10), channel_id=1, source_target_pairs={{0,8},{8,16},{16,24},{24,0},{1,9},{9,17},{17,25},{25,1},{2,10},{10... | collective-permute-start | bytes 1572872 | tf_op jit(solution)/shard_map/ppermute | solution.py:72
  575.9 43.9 %collective-permute-start.37 = (f32[2,1,128,512]{3,2,1,0:T(8,128)}, f32[2,1,128,512]{3,2,1,0:T(8,128)}, u32[]{:S(2)}, u32[]{:S(2)}) collective-permute-start(f32[2,1,128,512]{3,2,1,0:T(8,128)} %pad_maximum_fusion.9), channel_id=1, source_target_pairs={{0,16},{8,24},{16,0},{24,8},{1,17},{9,25},{17,1},{25,9},{2,18},{10... | collective-permute-start | bytes 1572872 | tf_op jit(solution)/shard_map/ppermute | solution.py:72
  582.5 38.9 %collective-permute-start.28 = (f32[2,1,128,512]{3,2,1,0:T(8,128)}, f32[2,1,128,512]{3,2,1,0:T(8,128)}, u32[]{:S(2)}, u32[]{:S(2)}) collective-permute-start(f32[2,1,128,512]{3,2,1,0:T(8,128)} %pad_maximum_fusion.8), channel_id=1, source_target_pairs={{0,24},{8,0},{16,8},{24,16},{1,25},{9,1},{17,9},{25,17},{2,26},{10... | collective-permute-start | bytes 1572872 | tf_op jit(solution)/shard_map/ppermute | solution.py:72
  586.6 45.8 %collective-permute-start.27 = (f32[2,1,128,512]{3,2,1,0:T(8,128)}, f32[2,1,128,512]{3,2,1,0:T(8,128)}, u32[]{:S(2)}, u32[]{:S(2)}) collective-permute-start(f32[2,1,128,512]{3,2,1,0:T(8,128)} %pad_maximum_fusion.7), channel_id=1, source_target_pairs={{0,8},{8,16},{16,24},{24,0},{1,9},{9,17},{17,25},{25,1},{2,10},{10... | collective-permute-start | bytes 1572872 | tf_op jit(solution)/shard_map/ppermute | solution.py:72
  607.2 56.5 %collective-permute-start.26 = (f32[2,1,128,512]{3,2,1,0:T(8,128)S(1)}, f32[2,1,128,512]{3,2,1,0:T(8,128)S(1)}, u32[]{:S(2)}, u32[]{:S(2)}) collective-permute-start(f32[2,1,128,512]{3,2,1,0:T(8,128)S(1)} %pad_maximum_fusion.6), channel_id=1, source_target_pairs={{0,16},{8,24},{16,0},{24,8},{1,17},{9,25},{17,1},{25,9},{2,18},{10... | collective-permute-start | bytes 1572872 | tf_op jit(solution)/shard_map/ppermute | solution.py:72
  (49 other events, 1161.6 us)
Sparse Core Ops, SparseCore 0:
  10.8 156.8 all-gather.2
  170.6 153.0 all-gather.4

commit v2 on v1

--- a/solution.py
+++ b/solution.py
@@ -85,43 +85,62 @@
                     + jnp.einsum(eq, rows[1], ws[1], preferred_element_type=f32))
 
         x_full = lax.all_gather(x_loc, ("tp", "dp"), axis=0, tiled=True)
-        gy_full = lax.all_gather(gy_loc, ("tp", "dp"), axis=0, tiled=True)
+        hd = d_model // 2
+        gy_full = lax.all_gather(gy_loc[:, :hd], ("tp", "dp"), axis=0, tiled=True)
+        gyb = exchange(lambda o: gy_loc[:, hd:])
+        gyb = place(0, gyb)
+        gyb_got = []
+        for o in (2, 1, 3):
+            gyb_got.append((o, lax.ppermute(gyb, "tp", [(i, (i + o) % tp_size) for i in range(tp_size)])))
+        gyb_rows = jnp.zeros((n_own, hd), bf16)
+        for o, v in [(0, gyb)] + gyb_got:
+            start = ((tz + tp_size - o) % tp_size) * (4 * tok)
+            gyb_rows = lax.dynamic_update_slice(gyb_rows, v, (start, 0))
         got_gu = exchange(lambda o: jnp.concatenate([quarter(wg_loc, 1, o), quarter(wu_loc, 1, o)], axis=1))
-        wd_late, got_gu[2], got_gu[4] = lax.optimization_barrier((wd_loc, got_gu[2], got_gu[4]))
-        got_d = exchange(lambda o: quarter(wd_late, 0, o))
+        got_d = exchange(lambda o: quarter(wd_loc, 0, o))
 
         wgu = place(0, got_gu)
         wgu = (wgu.reshape(4, d_loc, 2 * fq), swap(wgu, 1).reshape(4, d_loc, 2 * fq))
         wgu = jnp.where(core == 0, jnp.stack(wgu, axis=1), jnp.stack(wgu[::-1], axis=1)).reshape(d_model, 2 * fq)
-        x_full, got_d[2], got_d[4], got_d[6] = lax.optimization_barrier((x_full, got_d[2], got_d[4], got_d[6]))
         x_rows, x_cols = split_full(x_full)
         wd_all = place(1, got_d)
         wd_pair = (wd_all, swap(wd_all, 1))
-        wd_all = jnp.zeros((fq, d_model), bf16)
+        wd_all = [jnp.zeros((fq, hd), bf16) for _ in range(2)]
         for i in range(2):
             for c in range(4):
-                wd_all = lax.dynamic_update_slice(wd_all, wd_pair[i][:, c * d_loc:(c + 1) * d_loc],
-                                                  (0, (2 * c + (core + i) % 2) * d_loc))
+                wd_all[c // 2] = lax.dynamic_update_slice(wd_all[c // 2], wd_pair[i][:, c * d_loc:(c + 1) * d_loc],
+                                                          (0, (2 * (c % 2) + (core + i) % 2) * d_loc))
         pre = jnp.dot(x_rows, wgu, preferred_element_type=f32)
         gate_pre, up_pre = pre[:, :fq], pre[:, fq:]
         sig = jax.nn.sigmoid(gate_pre)
         silu = gate_pre * sig
         hidden = (silu * up_pre).astype(bf16).reshape(tp_size, 2, 2 * tok, fq)
-        got_h = far(*near(hidden[:, 0].reshape(half, fq), hidden[:, 1].reshape(half, fq)))
+        got_h = near(hidden[:, 0].reshape(half, fq), hidden[:, 1].reshape(half, fq))
+        got_h = far(*got_h)
         h_own = place(1, *got_h)
 
+        gy_full, gyb_rows, _ = lax.optimization_barrier((gy_full, gyb_rows, hidden))
         h_all = (h_own, swap(h_own, 1))
         y_part = [jnp.dot(h, wd_loc, preferred_element_type=f32) for h in h_all]
-        gy_full, _ = lax.optimization_barrier((gy_full, y_part))
         y_got = send_z([p.reshape(2, tp_size, 2 * tok, d_loc) for p in y_part])
-        gy_rows, gy_cols = split_full(gy_full)
-        grad_h = jnp.einsum("nd,fd->nf", gy_rows, wd_all, preferred_element_type=f32)
+        gya_rows = gy_full.reshape(tp_size, 2, 2, 2, tok, hd)
+        gya_rows = lax.dynamic_index_in_dim(gya_rows, core, 3, keepdims=False).reshape(n_own, hd)
+
+        def gy_col(dev):
+            start = (dev % 4) * d_loc
+            return jnp.where(dev < 4, lax.dynamic_slice_in_dim(gya_rows, start, d_loc, 1),
+                             lax.dynamic_slice_in_dim(gyb_rows, start, d_loc, 1))
+
+        gy_cols = [gy_col(me), swap(gy_col(me ^ 1), 1)]
+        gy_cols = [c.reshape(tp_size, 2, 2 * tok, d_loc).transpose(1, 0, 2, 3) for c in gy_cols]
+        grad_h = dot2((gya_rows, gyb_rows), wd_all, "nd,fd->nf")
         deriv = sig * (1.0 + gate_pre * (1.0 - sig))
         d_gate = (grad_h * up_pre * deriv).astype(bf16).reshape(tp_size, 2, 2 * tok, fq)
         d_up = (grad_h * silu).astype(bf16).reshape(tp_size, 2, 2 * tok, fq)
         got_0 = near(d_gate[:, 0].reshape(half, fq), d_up[:, 0].reshape(half, fq))
         got_1 = near(d_gate[:, 1].reshape(half, fq), d_up[:, 1].reshape(half, fq))
-        got_0, got_1 = far(*got_0), far(*got_1)
+        got_0 = far(*got_0)
+        got_1 = far(*got_1)
         grad_wd = dot2(h_all, [c.reshape(n_own, d_loc) for c in gy_cols], "nf,nd->fd")
 
         grad_wg = grad_wu = None
@@ -134,10 +153,11 @@
                     + jnp.einsum("nf,df->nd", du[i], wu_loc, preferred_element_type=f32) for i in range(2)]
             x_got.append(send_z([p.reshape(1, tp_size, 2 * tok, d_loc) for p in part]))
             xc = [c[y].reshape(half, d_loc) for c in x_cols]
-            part_g = dot2(xc, dg, "nd,nf->df")
-            part_u = dot2(xc, du, "nd,nf->df")
-            grad_wg = part_g if grad_wg is None else grad_wg + part_g
-            grad_wu = part_u if grad_wu is None else grad_wu + part_u
+            for i in range(2):
+                part_g = jnp.einsum("nd,nf->df", xc[i], dg[i], preferred_element_type=f32)
+                part_u = jnp.einsum("nd,nf->df", xc[i], du[i], preferred_element_type=f32)
+                grad_wg = part_g if grad_wg is None else grad_wg + part_g
+                grad_wu = part_u if grad_wu is None else grad_wu + part_u
         y_rows = finish(sum(y_got[1:], y_got[0]), x_cols)
         x_got = [sum(g[1:], g[0]) for g in x_got]
         gx_rows = finish(jnp.concatenate(x_got, axis=1), gy_cols)

time: 696 us -> 834 us (1.20)
  waiting for transfers between devices: 346 us -> 453 us
  starting transfers between devices: 49.6 us -> 88.3 us
  local copies, waits for them, and re-layouts: 117 us -> 90.6 us
  matrix products: 132 us -> 142 us
    ppermute x0 -> x3, waiting for transfers between devices: none -> 82.9 us  [local_step(): lax.ppermute(gyb, 'tp', [(i, (i + o) % tp_size) for i in range(tp_size)])]
    ppermute x9, waiting for transfers between devices: 78.1 us -> 109 us  [send_z(): got.append(lax.ppermute(blk(o), 'tp', perm))]
    all_to_all x2, waiting for transfers between devices: 29.4 us -> 0.01 us  [finish(): s = lax.all_to_all(s, 'dp', 0, 2, tiled=True)]
    dot_general x1 -> x8, matrix products: 16.4 us -> 45.1 us  [the longest x4 28.5 us: local_step(): part_u = jnp.einsum('nd,nf->df', xc[i], du[i], preferred_element_type=f32)]
    ppermute x9, starting transfers between devices: 13.4 us -> 38.7 us  [send_z(): got.append(lax.ppermute(blk(o), 'tp', perm))]
    ppermute x31 -> x35, waiting for transfers between devices: 237 us -> 260 us  [swap(): return lax.ppermute(v, 'dp', flip[o])]
    dot_general x5 -> x2, matrix products: 38.7 us -> 20.1 us  [dot2(): jnp.einsum(eq, rows[0], ws[0], preferred_element_type=f32)]
    dynamic_update_slice x31 -> x33, local copies, waits for them, and re-layouts: 42.8 us -> 28.2 us  [place(): out = lax.dynamic_update_slice(out, got[o], tuple(start))]
  transfers between devices with their start and end apart: 44 -> 51, of which waited for: 17 -> 21; matrix products, arithmetic and copies ran while one was open for 36% -> 32% of each run, Pallas kernels for 0% -> 0%
where the time goes in v2:
time: 834 us; the launch traced here: 827 us
  waiting for transfers between devices  453 us (54%)
  matrix products  142 us (17%)
  local copies, waits for them, and re-layouts  90.6 us (11%)
  starting transfers between devices  88.3 us (11%)
  other arithmetic  38.3 us (5%)
  between operations  15.6 us (2%)
    ppermute x35, waiting for transfers between devices, swap(): return lax.ppermute(v, 'dp', flip[o])  260 us
    ppermute x9, waiting for transfers between devices, send_z(): got.append(lax.ppermute(blk(o), 'tp', perm))  109 us
    ppermute x3, waiting for transfers between devices, local_step(): lax.ppermute(gyb, 'tp', [(i, (i + o) % tp_size) for i in range(tp_size)])  82.9 us
    ppermute x9, starting transfers between devices, send_z(): got.append(lax.ppermute(blk(o), 'tp', perm))  38.7 us
    ppermute x35, starting transfers between devices, swap(): return lax.ppermute(v, 'dp', flip[o])  34 us
    dot_general x4, matrix products, local_step(): part_u = jnp.einsum('nd,nf->df', xc[i], du[i], preferred_element_type=f32)  28.5 us
    dynamic_update_slice x33, local copies, waits for them, and re-layouts, place(): out = lax.dynamic_update_slice(out, got[o], tuple(start))  28.2 us
    dot_general x2, matrix products, dot2(): jnp.einsum(eq, rows[0], ws[0], preferred_element_type=f32)  20.1 us
  transfers between devices with their start and end apart: 51, of which 21 were waited for; matrix products, arithmetic and copies ran while one was open for 32% of the time, Pallas kernels for 0%

profile of v2, /device:TPU:0, one launch (start us, length us, event | category | flops | bytes accessed | tf_op | source)
XLA Modules:
  0.0 827.4 jit_solution(1070289272209672924)
XLA Ops:
  26.4 49.1 %collective-permute-done = bf16[512,1792]{1,0:T(8,128)(2,1)} collective-permute-done((bf16[512,1792]{1,0:T(8,128)(2,1)}, bf16[512,1792]{1,0:T(8,128)(2,1)}, u32[]{:S(2)}, u32[]{:S(2)}) %collective-permute-start) | collective-permute-done | bytes 1835040 | tf_op jit(solution)/shard_map/ppermute | solution.py:14
  81.4 55.3 %collective-permute-done.2 = bf16[512,1792]{1,0:T(8,128)(2,1)} collective-permute-done((bf16[512,1792]{1,0:T(8,128)(2,1)}, bf16[512,1792]{1,0:T(8,128)(2,1)}, u32[]{:S(2)}, u32[]{:S(2)}) %collective-permute-start.2) | collective-permute-done | bytes 1835040 | tf_op jit(solution)/shard_map/ppermute | solution.py:14
  146.9 19.7 %collective-permute-done.20 = bf16[896,512]{1,0:T(8,128)(2,1)S(1)} collective-permute-done((bf16[896,512]{1,0:T(8,128)(2,1)S(1)}, bf16[896,512]{1,0:T(8,128)(2,1)S(1)}, u32[]{:S(2)}, u32[]{:S(2)}) %collective-permute-start.20) | collective-permute-done | bytes 917536 | tf_op jit(solution)/shard_map/ppermute | solution.py:14
  167.6 21.8 %collective-permute-done.21 = bf16[896,512]{1,0:T(8,128)(2,1)S(1)} collective-permute-done((bf16[896,512]{1,0:T(8,128)(2,1)S(1)}, bf16[896,512]{1,0:T(8,128)(2,1)S(1)}, u32[]{:S(2)}, u32[]{:S(2)}) %collective-permute-start.21) | collective-permute-done | bytes 917536 | tf_op jit(solution)/shard_map/ppermute | solution.py:14
  194.9 5.7 collective-permute-done.14
  200.7 5.9 collective-permute-done.15
  220.0 82.9 %collective-permute-done.17 = bf16[256,2048]{1,0:T(8,128)(2,1)S(1)} collective-permute-done((bf16[256,2048]{1,0:T(8,128)(2,1)S(1)}, bf16[256,2048]{1,0:T(8,128)(2,1)S(1)}, u32[]{:S(2)}, u32[]{:S(2)}) %collective-permute-start.17) | collective-permute-done | bytes 1048608 | tf_op jit(solution)/shard_map/ppermute | solution.py:94
  311.1 17.5 %maximum_select_fusion = bf16[4,2,512,1792]{3,2,1,0:T(8,128)(2,1)} fusion(bf16[4,1,512,1792]{3,2,1,0:T(8,128)(2,1)} %bitcast.3, bf16[4,1,512,1792]{3,2,1,0:T(8,128)(2,1)} %bitcast.2, pred[]{:T(512)S(6)} %eq.47), kind=kLoop, calls=%fused_computation | loop fusion | flops 22020096 | bytes 29360128 | tf_op jit(solution)/shard_map/jit(_where)/select_n | solution.py:104
  328.6 7.7 constant_dynamic-slice_fusion.34
  336.3 19.0 %fusion.16 = f32[1024,1792]{1,0:T(8,128)S(1)} fusion(bf16[1024,4096]{1,0:T(8,128)(2,1)} %bitcast.139, bf16[4096,1792]{1,0:T(8,128)(2,1)} %bitcast.136), kind=kOutput, calls=%fused_computation.140 | convolution fusion | flops 15032385536 | bytes 30408704 | tf_op jit(solution)/shard_map/dot_general | solution.py:113
  371.7 8.7 %fusion.19 = f32[1024,896]{1,0:T(8,128)} fusion(bf16[1024,2048]{1,0:T(8,128)(2,1)S(1)} %copy-done.4, bf16[896,2048]{1,0:T(8,128)(2,1)} %copy-done.16), kind=kOutput, calls=%fused_computation.143 | convolution fusion | flops 3758096384 | bytes 11534336 | tf_op jit(solution)/shard_map/nd,fd->nf/dot_general | solution.py:85
  380.4 9.8 %multiply_convert_fusion.1 = (bf16[1024,896]{1,0:T(8,128)(2,1)S(1)}, bf16[1024,896]{1,0:T(8,128)(2,1)}) fusion(f32[1024,1792]{1,0:T(8,128)S(1)} %bitcast.141, f32[1024,896]{1,0:T(8,128)} %fusion.19, bf16[1024,2048]{1,0:T(8,128)(2,1)S(1)} %bitcast.137, bf16[896,2048]{1,0:T(8,128)(2,1)} %copy-done.17), kind=kOutput, calls=%fused_computation.5 | convolution fusion | flops 3770941440 | bytes 22544384 | tf_op jit(solution)/shard_map/nd,fd->nf/dot_general | solution.py:84
  406.3 14.9 %collective-permute-done.38 = bf16[512,896]{1,0:T(8,128)(2,1)S(1)} collective-permute-done((bf16[512,896]{1,0:T(8,128)(2,1)S(1)}, bf16[512,896]{1,0:T(8,128)(2,1)S(1)}, u32[]{:S(2)}, u32[]{:S(2)}) %collective-permute-start.38) | collective-permute-done | bytes 917536 | tf_op jit(solution)/shard_map/ppermute | solution.py:14
  432.3 8.5 %collective-permute-done.35 = bf16[512,896]{1,0:T(8,128)(2,1)S(1)} collective-permute-done((bf16[512,896]{1,0:T(8,128)(2,1)S(1)}, bf16[512,896]{1,0:T(8,128)(2,1)S(1)}, u32[]{:S(2)}, u32[]{:S(2)}) %collective-permute-start.35) | collective-permute-done | bytes 917536 | tf_op jit(solution)/shard_map/ppermute | solution.py:14
  443.0 17.5 %collective-permute-done.27 = bf16[512,896]{1,0:T(8,128)(2,1)S(1)} collective-permute-done((bf16[512,896]{1,0:T(8,128)(2,1)S(1)}, bf16[512,896]{1,0:T(8,128)(2,1)S(1)}, u32[]{:S(2)}, u32[]{:S(2)}) %collective-permute-start.27) | collective-permute-done | bytes 917536 | tf_op jit(solution)/shard_map/ppermute | solution.py:14
  463.1 17.1 %collective-permute-done.24 = bf16[512,896]{1,0:T(8,128)(2,1)S(1)} collective-permute-done((bf16[512,896]{1,0:T(8,128)(2,1)S(1)}, bf16[512,896]{1,0:T(8,128)(2,1)S(1)}, u32[]{:S(2)}, u32[]{:S(2)}) %collective-permute-start.24) | collective-permute-done | bytes 917536 | tf_op jit(solution)/shard_map/ppermute | solution.py:14
  486.4 15.3 %collective-permute-done.8 = bf16[512,896]{1,0:T(8,128)(2,1)S(1)} collective-permute-done((bf16[512,896]{1,0:T(8,128)(2,1)}, bf16[512,896]{1,0:T(8,128)(2,1)S(1)}, u32[]{:S(2)}, u32[]{:S(2)}) %collective-permute-start.8) | collective-permute-done | bytes 917536 | tf_op jit(solution)/shard_map/ppermute | solution.py:14
  504.3 15.2 %collective-permute-done.40 = bf16[512,896]{1,0:T(8,128)(2,1)S(1)} collective-permute-done((bf16[512,896]{1,0:T(8,128)(2,1)S(1)}, bf16[512,896]{1,0:T(8,128)(2,1)S(1)}, u32[]{:S(2)}, u32[]{:S(2)}) %collective-permute-start.40) | collective-permute-done | bytes 917536 | tf_op jit(solution)/shard_map/ppermute | solution.py:14
  522.5 12.8 %collective-permute-done.29 = bf16[512,896]{1,0:T(8,128)(2,1)S(1)} collective-permute-done((bf16[512,896]{1,0:T(8,128)(2,1)S(1)}, bf16[512,896]{1,0:T(8,128)(2,1)S(1)}, u32[]{:S(2)}, u32[]{:S(2)}) %collective-permute-start.29) | collective-permute-done | bytes 917536 | tf_op jit(solution)/shard_map/ppermute | solution.py:14
  543.6 6.5 fusion.17
  563.1 5.5 fusion.23
  573.3 29.2 %collective-permute-start.44 = (f32[2,1,128,512]{3,2,1,0:T(8,128)}, f32[2,1,128,512]{3,2,1,0:T(8,128)}, u32[]{:S(2)}, u32[]{:S(2)}) collective-permute-start(f32[2,1,128,512]{3,2,1,0:T(8,128)} %pad_maximum_fusion.10), channel_id=1, source_target_pairs={{0,8},{8,16},{16,24},{24,0},{1,9},{9,17},{17,25},{25,1},{2,10},{10... | collective-permute-start | bytes 1572872 | tf_op jit(solution)/shard_map/ppermute | solution.py:72
  623.1 8.2 add_add_fusion.1
  631.3 7.5 fusion.29
  652.0 10.6 %collective-permute-done.33 = f32[2,1,128,512]{3,2,1,0:T(8,128)S(1)} collective-permute-done((f32[2,1,128,512]{3,2,1,0:T(8,128)S(1)}, f32[2,1,128,512]{3,2,1,0:T(8,128)S(1)}, u32[]{:S(2)}, u32[]{:S(2)}) %collective-permute-start.33) | collective-permute-done | bytes 524320 | tf_op jit(solution)/shard_map/ppermute | solution.py:72
  662.6 31.4 %collective-permute-done.32 = f32[2,1,128,512]{3,2,1,0:T(8,128)S(1)} collective-permute-done((f32[2,1,128,512]{3,2,1,0:T(8,128)S(1)}, f32[2,1,128,512]{3,2,1,0:T(8,128)S(1)}, u32[]{:S(2)}, u32[]{:S(2)}) %collective-permute-start.32) | collective-permute-done | bytes 524320 | tf_op jit(solution)/shard_map/ppermute | solution.py:72
  700.9 7.4 fusion.18
  714.8 10.9 %add_add_fusion = f32[512,3584]{1,0:T(8,128)} fusion(f32[512,3584]{1,0:T(8,128)} %fusion.29, f32[512,3584]{1,0:T(8,128)S(1)} %bitcast.135, f32[512,3584]{1,0:T(8,128)} %fusion.28, bf16[512,512]{1,0:T(8,128)(2,1)S(1)} %bitcast.152, bf16[512,3584]{1,0:T(8,128)(2,1)S(1)} %copy-done.1), kind=kOutput, calls=%fused_computation.1 | convolution fusion | flops 1884553216 | bytes 33554432 | tf_op jit(solution)/shard_map/nd,nf->df/dot_general | solution.py:158
  727.6 10.5 %fusion.30 = f32[3584,512]{1,0:T(8,128)} fusion(bf16[1024,3584]{1,0:T(8,128)(2,1)} %collective-permute-done.10, bf16[1024,512]{1,0:T(8,128)(2,1)} %bitcast.193), kind=kOutput, calls=%fused_computation.154 | convolution fusion | flops 3758096384 | bytes 15728640 | tf_op jit(solution)/shard_map/nf,nd->fd/dot_general | solution.py:85
  738.1 21.9 %collective-permute-done.13 = f32[2,2,128,512]{3,2,1,0:T(8,128)} collective-permute-done((f32[2,2,128,512]{3,2,1,0:T(8,128)}, f32[2,2,128,512]{3,2,1,0:T(8,128)}, u32[]{:S(2)}, u32[]{:S(2)}) %collective-permute-start.13) | collective-permute-done | bytes 1048608 | tf_op jit(solution)/shard_map/ppermute | solution.py:72
  760.0 41.7 %collective-permute-done.11 = f32[2,2,128,512]{3,2,1,0:T(8,128)} collective-permute-done((f32[2,2,128,512]{3,2,1,0:T(8,128)}, f32[2,2,128,512]{3,2,1,0:T(8,128)}, u32[]{:S(2)}, u32[]{:S(2)}) %collective-permute-start.11) | collective-permute-done | bytes 1048608 | tf_op jit(solution)/shard_map/ppermute | solution.py:72
  808.9 10.3 %convolution_add_fusion = f32[3584,512]{1,0:T(8,128)} fusion(f32[3584,512]{1,0:T(8,128)} %fusion.30, bf16[1024,3584]{1,0:T(8,128)(2,1)} %constant_dynamic-update-slice_fusion.34, bf16[1024,512]{1,0:T(8,128)(2,1)S(1)} %bitcast.192), kind=kOutput, calls=%fused_computation.3 | convolution fusion | flops 3759931392 | bytes 23068672 | tf_op jit(solution)/shard_map/nf,nd->fd/dot_general | solution.py:84
  (301 shorter events, 205.7 us)
Async XLA Ops:
  7.2 321.5 %all-gather.3.cloned.1.call-start = ((), (), s32[]{:S(2)}) async-start(), calls=%async_computation.2 | async-start | bytes 17301504 | tf_op jit(solution)/shard_map/all_gather | solution.py:87
  7.9 360.4 %all-gather.5.cloned.1.call-start = ((), (), s32[]{:S(2)}) async-start(), calls=%async_computation.3 | async-start | bytes 8650752 | tf_op jit(solution)/shard_map/all_gather | solution.py:89
  13.3 62.3 %collective-permute-start = (bf16[512,1792]{1,0:T(8,128)(2,1)}, bf16[512,1792]{1,0:T(8,128)(2,1)}, u32[]{:S(2)}, u32[]{:S(2)}) collective-permute-start(bf16[512,1792]{1,0:T(8,128)(2,1)} %pad_maximum_fusion), channel_id=1, source_target_pairs={{0,2},{1,3},{2,0},{3,1},{4,6},{5,7},{6,4},{7,5},{8,10},{9,11},{10,... | collective-permute-start | bytes 5505032 | tf_op jit(solution)/shard_map/ppermute | solution.py:14
  17.6 60.9 %collective-permute-start.1 = (bf16[512,1792]{1,0:T(8,128)(2,1)}, bf16[512,1792]{1,0:T(8,128)(2,1)}, u32[]{:S(2)}, u32[]{:S(2)}) collective-permute-start(bf16[512,1792]{1,0:T(8,128)(2,1)} %pad_maximum_fusion.1), channel_id=1, source_target_pairs={{0,4},{1,5},{2,6},{3,7},{4,0},{5,1},{6,2},{7,3},{8,12},{9,13},{10,... | collective-permute-start | bytes 5505032 | tf_op jit(solution)/shard_map/ppermute | solution.py:14
  20.5 116.2 %collective-permute-start.2 = (bf16[512,1792]{1,0:T(8,128)(2,1)}, bf16[512,1792]{1,0:T(8,128)(2,1)}, u32[]{:S(2)}, u32[]{:S(2)}) collective-permute-start(bf16[512,1792]{1,0:T(8,128)(2,1)} %pad_maximum_fusion.2), channel_id=1, source_target_pairs={{0,6},{1,7},{2,4},{3,5},{4,2},{5,3},{6,0},{7,1},{8,14},{9,15},{10,... | collective-permute-start | bytes 5505032 | tf_op jit(solution)/shard_map/ppermute | solution.py:14
  139.5 169.8 %collective-permute-start.3 = (bf16[2048,1792]{1,0:T(8,128)(2,1)}, bf16[2048,1792]{1,0:T(8,128)(2,1)}, u32[]{:S(2)}, u32[]{:S(2)}) collective-permute-start(bf16[2048,1792]{1,0:T(8,128)(2,1)} %constant_dynamic-update-slice_fusion.31), channel_id=1, source_target_pairs={{0,1},{1,0},{2,3},{3,2},{4,5},{5,4},{6,7},{7,6},{8,9},{9,8},{10,11... | collective-permute-start | bytes 22020104 | tf_op jit(solution)/shard_map/ppermute | solution.py:14
  145.5 44.0 %collective-permute-start.21 = (bf16[896,512]{1,0:T(8,128)(2,1)S(1)}, bf16[896,512]{1,0:T(8,128)(2,1)S(1)}, u32[]{:S(2)}, u32[]{:S(2)}) collective-permute-start(bf16[896,512]{1,0:T(8,128)(2,1)S(1)} %get-tuple-element.22), channel_id=1, source_target_pairs={{0,4},{1,5},{2,6},{3,7},{4,0},{5,1},{6,2},{7,3},{8,12},{9,13},{10,... | collective-permute-start | bytes 2752520 | tf_op jit(solution)/shard_map/ppermute | solution.py:14
  146.2 44.3 %collective-permute-start.22 = (bf16[896,512]{1,0:T(8,128)(2,1)S(1)}, bf16[896,512]{1,0:T(8,128)(2,1)S(1)}, u32[]{:S(2)}, u32[]{:S(2)}) collective-permute-start(bf16[896,512]{1,0:T(8,128)(2,1)S(1)} %get-tuple-element.19), channel_id=1, source_target_pairs={{0,6},{1,7},{2,4},{3,5},{4,2},{5,3},{6,0},{7,1},{8,14},{9,15},{10,... | collective-permute-start | bytes 2752520 | tf_op jit(solution)/shard_map/ppermute | solution.py:14
  191.4 111.9 %collective-permute-start.23 = (bf16[896,2048]{1,0:T(8,128)(2,1)}, bf16[896,2048]{1,0:T(8,128)(2,1)}, u32[]{:S(2)}, u32[]{:S(2)}) collective-permute-start(bf16[896,2048]{1,0:T(8,128)(2,1)} %constant_dynamic-update-slice_fusion.16), channel_id=1, source_target_pairs={{0,1},{1,0},{2,3},{3,2},{4,5},{5,4},{6,7},{7,6},{8,9},{9,8},{10,11... | collective-permute-start | bytes 11010056 | tf_op jit(solution)/shard_map/ppermute | solution.py:14
  206.6 96.3 %collective-permute-start.17 = (bf16[256,2048]{1,0:T(8,128)(2,1)S(1)}, bf16[256,2048]{1,0:T(8,128)(2,1)S(1)}, u32[]{:S(2)}, u32[]{:S(2)}) collective-permute-start(bf16[256,2048]{1,0:T(8,128)(2,1)S(1)} %constant_dynamic-update-slice_fusion.23), channel_id=1, source_target_pairs={{0,16},{8,24},{16,0},{24,8},{1,17},{9,25},{17,1},{25,9},{2,18},{10... | collective-permute-start | bytes 3145736 | tf_op jit(solution)/shard_map/ppermute | solution.py:94
  210.1 92.9 %collective-permute-start.18 = (bf16[256,2048]{1,0:T(8,128)(2,1)S(1)}, bf16[256,2048]{1,0:T(8,128)(2,1)S(1)}, u32[]{:S(2)}, u32[]{:S(2)}) collective-permute-start(bf16[256,2048]{1,0:T(8,128)(2,1)S(1)} %constant_dynamic-update-slice_fusion.23), channel_id=1, source_target_pairs={{0,8},{8,16},{16,24},{24,0},{1,9},{9,17},{17,25},{25,1},{2,10},{10... | collective-permute-start | bytes 3145736 | tf_op jit(solution)/shard_map/ppermute | solution.py:94
  211.8 91.3 %collective-permute-start.19 = (bf16[256,2048]{1,0:T(8,128)(2,1)S(1)}, bf16[256,2048]{1,0:T(8,128)(2,1)S(1)}, u32[]{:S(2)}, u32[]{:S(2)}) collective-permute-start(bf16[256,2048]{1,0:T(8,128)(2,1)S(1)} %constant_dynamic-update-slice_fusion.23), channel_id=1, source_target_pairs={{0,24},{8,0},{16,8},{24,16},{1,25},{9,1},{17,9},{25,17},{2,26},{10... | collective-permute-start | bytes 3145736 | tf_op jit(solution)/shard_map/ppermute | solution.py:94
  360.3 43.0 %collective-permute-start.6 = (bf16[512,896]{1,0:T(8,128)(2,1)S(1)}, bf16[512,896]{1,0:T(8,128)(2,1)}, u32[]{:S(2)}, u32[]{:S(2)}) collective-permute-start(bf16[512,896]{1,0:T(8,128)(2,1)S(1)} %bitcast.169), channel_id=1, source_target_pairs={{0,4},{1,5},{2,6},{3,7},{4,0},{5,1},{6,2},{7,3},{8,12},{9,13},{10,... | collective-permute-start | bytes 2752520 | tf_op jit(solution)/shard_map/ppermute | solution.py:14
  362.4 41.6 %collective-permute-start.7 = (bf16[512,896]{1,0:T(8,128)(2,1)S(1)}, bf16[512,896]{1,0:T(8,128)(2,1)}, u32[]{:S(2)}, u32[]{:S(2)}) collective-permute-start(bf16[512,896]{1,0:T(8,128)(2,1)S(1)} %bitcast.166), channel_id=1, source_target_pairs={{0,4},{1,5},{2,6},{3,7},{4,0},{5,1},{6,2},{7,3},{8,12},{9,13},{10,... | collective-permute-start | bytes 2752520 | tf_op jit(solution)/shard_map/ppermute | solution.py:14
  404.0 56.5 %collective-permute-start.27 = (bf16[512,896]{1,0:T(8,128)(2,1)S(1)}, bf16[512,896]{1,0:T(8,128)(2,1)S(1)}, u32[]{:S(2)}, u32[]{:S(2)}) collective-permute-start(bf16[512,896]{1,0:T(8,128)(2,1)S(1)} %bitcast.163), channel_id=1, source_target_pairs={{0,2},{1,3},{2,0},{3,1},{4,6},{5,7},{6,4},{7,5},{8,10},{9,11},{10,... | collective-permute-start | bytes 2752520 | tf_op jit(solution)/shard_map/ppermute | solution.py:14
  421.2 41.2 %collective-permute-start.28 = (bf16[512,896]{1,0:T(8,128)(2,1)S(1)}, bf16[512,896]{1,0:T(8,128)(2,1)S(1)}, u32[]{:S(2)}, u32[]{:S(2)}) collective-permute-start(bf16[512,896]{1,0:T(8,128)(2,1)S(1)} %bitcast.164), channel_id=1, source_target_pairs={{0,4},{1,5},{2,6},{3,7},{4,0},{5,1},{6,2},{7,3},{8,12},{9,13},{10,... | collective-permute-start | bytes 2752520 | tf_op jit(solution)/shard_map/ppermute | solution.py:14
  425.2 55.0 %collective-permute-start.24 = (bf16[512,896]{1,0:T(8,128)(2,1)S(1)}, bf16[512,896]{1,0:T(8,128)(2,1)S(1)}, u32[]{:S(2)}, u32[]{:S(2)}) collective-permute-start(bf16[512,896]{1,0:T(8,128)(2,1)S(1)} %bitcast.160), channel_id=1, source_target_pairs={{0,2},{1,3},{2,0},{3,1},{4,6},{5,7},{6,4},{7,5},{8,10},{9,11},{10,... | collective-permute-start | bytes 2752520 | tf_op jit(solution)/shard_map/ppermute | solution.py:14
  440.8 41.4 %collective-permute-start.25 = (bf16[512,896]{1,0:T(8,128)(2,1)S(1)}, bf16[512,896]{1,0:T(8,128)(2,1)S(1)}, u32[]{:S(2)}, u32[]{:S(2)}) collective-permute-start(bf16[512,896]{1,0:T(8,128)(2,1)S(1)} %bitcast.161), channel_id=1, source_target_pairs={{0,4},{1,5},{2,6},{3,7},{4,0},{5,1},{6,2},{7,3},{8,12},{9,13},{10,... | collective-permute-start | bytes 2752520 | tf_op jit(solution)/shard_map/ppermute | solution.py:14
  460.5 41.2 %collective-permute-start.8 = (bf16[512,896]{1,0:T(8,128)(2,1)}, bf16[512,896]{1,0:T(8,128)(2,1)S(1)}, u32[]{:S(2)}, u32[]{:S(2)}) collective-permute-start(bf16[512,896]{1,0:T(8,128)(2,1)} %collective-permute-done.4), channel_id=1, source_target_pairs={{0,4},{1,5},{2,6},{3,7},{4,0},{5,1},{6,2},{7,3},{8,12},{9,13},{10,... | collective-permute-start | bytes 2752520 | tf_op jit(solution)/shard_map/ppermute | solution.py:14
  483.1 52.3 %collective-permute-start.29 = (bf16[512,896]{1,0:T(8,128)(2,1)S(1)}, bf16[512,896]{1,0:T(8,128)(2,1)S(1)}, u32[]{:S(2)}, u32[]{:S(2)}) collective-permute-start(bf16[512,896]{1,0:T(8,128)(2,1)S(1)} %collective-permute-done.28), channel_id=1, source_target_pairs={{0,2},{1,3},{2,0},{3,1},{4,6},{5,7},{6,4},{7,5},{8,10},{9,11},{10,... | collective-permute-start | bytes 2752520 | tf_op jit(solution)/shard_map/ppermute | solution.py:14
  504.3 196.5 %collective-permute-start.10 = (bf16[1024,3584]{1,0:T(8,128)(2,1)}, bf16[1024,3584]{1,0:T(8,128)(2,1)}, u32[]{:S(2)}, u32[]{:S(2)}) collective-permute-start(bf16[1024,3584]{1,0:T(8,128)(2,1)} %constant_dynamic-update-slice_fusion.34), channel_id=1, source_target_pairs={{0,1},{1,0},{2,3},{3,2},{4,5},{5,4},{6,7},{7,6},{8,9},{9,8},{10,11... | collective-permute-start | bytes 22020104 | tf_op jit(solution)/shard_map/ppermute | solution.py:14
  519.6 43.5 %collective-permute-start.42 = (bf16[512,3584]{1,0:T(8,128)(2,1)S(1)}, bf16[512,3584]{1,0:T(8,128)(2,1)S(1)}, u32[]{:S(2)}, u32[]{:S(2)}) collective-permute-start(bf16[512,3584]{1,0:T(8,128)(2,1)S(1)} %constant_dynamic-update-slice_fusion), channel_id=1, source_target_pairs={{0,1},{1,0},{2,3},{3,2},{4,5},{5,4},{6,7},{7,6},{8,9},{9,8},{10,11... | collective-permute-start | bytes 11010056 | tf_op jit(solution)/shard_map/ppermute | solution.py:14
  522.0 46.7 %collective-permute-start.41 = (bf16[512,3584]{1,0:T(8,128)(2,1)S(1)}, bf16[512,3584]{1,0:T(8,128)(2,1)S(1)}, u32[]{:S(2)}, u32[]{:S(2)}) collective-permute-start(bf16[512,3584]{1,0:T(8,128)(2,1)S(1)} %constant_dynamic-update-slice_fusion.4), channel_id=1, source_target_pairs={{0,1},{1,0},{2,3},{3,2},{4,5},{5,4},{6,7},{7,6},{8,9},{9,8},{10,11... | collective-permute-start | bytes 11010056 | tf_op jit(solution)/shard_map/ppermute | solution.py:14
  535.5 67.9 %collective-permute-start.31 = (bf16[512,3584]{1,0:T(8,128)(2,1)S(1)}, bf16[512,3584]{1,0:T(8,128)(2,1)S(1)}, u32[]{:S(2)}, u32[]{:S(2)}) collective-permute-start(bf16[512,3584]{1,0:T(8,128)(2,1)S(1)} %constant_dynamic-update-slice_fusion.8), channel_id=1, source_target_pairs={{0,1},{1,0},{2,3},{3,2},{4,5},{5,4},{6,7},{7,6},{8,9},{9,8},{10,11... | collective-permute-start | bytes 11010056 | tf_op jit(solution)/shard_map/ppermute | solution.py:14
  539.0 69.9 %collective-permute-start.30 = (bf16[512,3584]{1,0:T(8,128)(2,1)S(1)}, bf16[512,3584]{1,0:T(8,128)(2,1)}, u32[]{:S(2)}, u32[]{:S(2)}) collective-permute-start(bf16[512,3584]{1,0:T(8,128)(2,1)S(1)} %constant_dynamic-update-slice_fusion.12), channel_id=1, source_target_pairs={{0,1},{1,0},{2,3},{3,2},{4,5},{5,4},{6,7},{7,6},{8,9},{9,8},{10,11... | collective-permute-start | bytes 11010056 | tf_op jit(solution)/shard_map/ppermute | solution.py:14
  572.4 66.5 %collective-permute-start.45 = (f32[2,1,128,512]{3,2,1,0:T(8,128)}, f32[2,1,128,512]{3,2,1,0:T(8,128)}, u32[]{:S(2)}, u32[]{:S(2)}) collective-permute-start(f32[2,1,128,512]{3,2,1,0:T(8,128)} %pad_maximum_fusion.11), channel_id=1, source_target_pairs={{0,24},{8,0},{16,8},{24,16},{1,25},{9,1},{17,9},{25,17},{2,26},{10... | collective-permute-start | bytes 1572872 | tf_op jit(solution)/shard_map/ppermute | solution.py:72
  573.3 66.8 %collective-permute-start.44 = (f32[2,1,128,512]{3,2,1,0:T(8,128)}, f32[2,1,128,512]{3,2,1,0:T(8,128)}, u32[]{:S(2)}, u32[]{:S(2)}) collective-permute-start(f32[2,1,128,512]{3,2,1,0:T(8,128)} %pad_maximum_fusion.10), channel_id=1, source_target_pairs={{0,8},{8,16},{16,24},{24,0},{1,9},{9,17},{17,25},{25,1},{2,10},{10... | collective-permute-start | bytes 1572872 | tf_op jit(solution)/shard_map/ppermute | solution.py:72
  603.3 47.0 %collective-permute-start.43 = (f32[2,1,128,512]{3,2,1,0:T(8,128)}, f32[2,1,128,512]{3,2,1,0:T(8,128)}, u32[]{:S(2)}, u32[]{:S(2)}) collective-permute-start(f32[2,1,128,512]{3,2,1,0:T(8,128)} %pad_maximum_fusion.9), channel_id=1, source_target_pairs={{0,16},{8,24},{16,0},{24,8},{1,17},{9,25},{17,1},{25,9},{2,18},{10... | collective-permute-start | bytes 1572872 | tf_op jit(solution)/shard_map/ppermute | solution.py:72
  640.0 54.0 %collective-permute-start.32 = (f32[2,1,128,512]{3,2,1,0:T(8,128)S(1)}, f32[2,1,128,512]{3,2,1,0:T(8,128)S(1)}, u32[]{:S(2)}, u32[]{:S(2)}) collective-permute-start(f32[2,1,128,512]{3,2,1,0:T(8,128)S(1)} %pad_maximum_fusion.6), channel_id=1, source_target_pairs={{0,16},{8,24},{16,0},{24,8},{1,17},{9,25},{17,1},{25,9},{2,18},{10... | collective-permute-start | bytes 1572872 | tf_op jit(solution)/shard_map/ppermute | solution.py:72
  710.4 49.6 %collective-permute-start.13 = (f32[2,2,128,512]{3,2,1,0:T(8,128)}, f32[2,2,128,512]{3,2,1,0:T(8,128)}, u32[]{:S(2)}, u32[]{:S(2)}) collective-permute-start(f32[2,2,128,512]{3,2,1,0:T(8,128)} %pad_maximum_fusion.5), channel_id=1, source_target_pairs={{0,24},{8,0},{16,8},{24,16},{1,25},{9,1},{17,9},{25,17},{2,26},{10... | collective-permute-start | bytes 3145736 | tf_op jit(solution)/shard_map/ppermute | solution.py:72
  711.7 48.2 %collective-permute-start.12 = (f32[2,2,128,512]{3,2,1,0:T(8,128)}, f32[2,2,128,512]{3,2,1,0:T(8,128)}, u32[]{:S(2)}, u32[]{:S(2)}) collective-permute-start(f32[2,2,128,512]{3,2,1,0:T(8,128)} %pad_maximum_fusion.4), channel_id=1, source_target_pairs={{0,8},{8,16},{16,24},{24,0},{1,9},{9,17},{17,25},{25,1},{2,10},{10... | collective-permute-start | bytes 3145736 | tf_op jit(solution)/shard_map/ppermute | solution.py:72
  714.8 86.9 %collective-permute-start.11 = (f32[2,2,128,512]{3,2,1,0:T(8,128)}, f32[2,2,128,512]{3,2,1,0:T(8,128)}, u32[]{:S(2)}, u32[]{:S(2)}) collective-permute-start(f32[2,2,128,512]{3,2,1,0:T(8,128)} %pad_maximum_fusion.3), channel_id=1, source_target_pairs={{0,16},{8,24},{16,0},{24,8},{1,17},{9,25},{17,1},{25,9},{2,18},{10... | collective-permute-start | bytes 3145736 | tf_op jit(solution)/shard_map/ppermute | solution.py:72
  (70 other events, 2192.5 us)
Sparse Core Ops, SparseCore 0:
  10.8 156.1 all-gather.2
  170.5 140.9 all-gather.4
